TPU v7x, 32 devices: a whole 2x2x4 slice. The times are simulated.
32 devices in a mesh: pp: 4 (over z), dp: 8 (over y, x, core).
Axes of the slice: x: 2, y: 2, z: 4, core: 2. Of those that a mesh axis runs over, the one named last changes fastest.
Arguments:
- w_in: bfloat16 [4, 2, 768, 3072], P('pp')
- w_out: bfloat16 [4, 2, 3072, 768], P('pp')
- x_saved: bfloat16 [4, 4, 2, 512, 768], P('pp', None, None, 'dp')
- h_saved: bfloat16 [4, 4, 2, 512, 3072], P('pp', None, None, 'dp')
- dy_in: bfloat16 [4, 512, 768], P('pp', 'dp')
- acc_in: float32 [4, 8, 2, 768, 3072], P('pp', 'dp')
- acc_out: float32 [4, 8, 2, 3072, 768], P('pp', 'dp')
Outputs:
- output 1: float32 [4, 2, 768, 3072], P('pp')
- output 2: float32 [4, 2, 3072, 768], P('pp')
- output 3: bfloat16 [4, 512, 768], P('pp', 'dp')
All inputs are finite; a program needn't handle non-finite values.
Results may differ from a plain program's by a relative error of at most 0.0112023.
Values are sent between devices in bfloat16 or wider.
A program may use at most 1 GiB of HBM per device.

v0:
```python
import functools
import jax
import jax.numpy as jnp
from jax import lax
from jax.sharding import PartitionSpec as P


def layer_backward(w_first, w_second, x_in, h_pre, cot_in):
    act_val, act_vjp = jax.vjp(jax.nn.gelu, h_pre.astype(jnp.float32))
    act_bf = act_val.astype(jnp.bfloat16)
    d_act = lax.dot_general(cot_in, w_second, (((1,), (1,)), ((), ())), preferred_element_type=jnp.float32)
    d_pre = act_vjp(d_act)[0].astype(jnp.bfloat16)
    grad_first = lax.dot_general(x_in, d_pre, (((0,), (0,)), ((), ())), preferred_element_type=jnp.float32)
    grad_second = lax.dot_general(act_bf, cot_in, (((0,), (0,)), ((), ())), preferred_element_type=jnp.float32)
    back_sum = lax.dot_general(d_pre, w_first, (((1,), (1,)), ((), ())), preferred_element_type=jnp.float32)
    cot_out = (cot_in.astype(jnp.float32) + back_sum).astype(jnp.bfloat16)
    return cot_out, grad_first, grad_second


def solution(mesh):
    stages = mesh.shape['pp']
    replicas = mesh.shape['dp']
    down_pairs = [(sender, sender - 1) for sender in range(1, stages)]

    def device_fn(w_in, w_out, x_saved, h_saved, dy_in, acc_in, acc_out):
        stage_id = lax.axis_index('pp')
        w_first = w_in[0]
        w_second = w_out[0]
        layers = w_first.shape[0]
        x_local = x_saved[0]
        h_local = h_saved[0]

        def backward_slot(slot_id, operands):
            cot_cur, acc_first, acc_second = operands
            new_first = list(acc_first)
            new_second = list(acc_second)
            x_slot = lax.dynamic_index_in_dim(x_local, slot_id, 0, keepdims=False)
            h_slot = lax.dynamic_index_in_dim(h_local, slot_id, 0, keepdims=False)
            for layer_id in reversed(range(layers)):
                cot_cur, grad_first, grad_second = layer_backward(w_first[layer_id], w_second[layer_id], x_slot[layer_id], h_slot[layer_id], cot_cur)
                new_first[layer_id] = new_first[layer_id] + grad_first
                new_second[layer_id] = new_second[layer_id] + grad_second
            return cot_cur, new_first, new_second

        def run_step(slot_id, loop_state):
            cot_cur, acc_first, acc_second, dx_all = loop_state
            cot_cur, acc_first, acc_second = lax.cond(stage_id + slot_id < stages, functools.partial(backward_slot, slot_id), lambda operands: operands, (cot_cur, acc_first, acc_second))
            dx_all = lax.dynamic_update_index_in_dim(dx_all, cot_cur, slot_id, 0)
            return cot_cur, acc_first, acc_second, dx_all

        def loop_body(slot_id, loop_state):
            cot_cur, acc_first, acc_second, dx_all = run_step(slot_id, loop_state)
            cot_next = lax.ppermute(cot_cur, 'pp', perm=down_pairs)
            return cot_next, acc_first, acc_second, dx_all

        acc_first = [acc_in[0, 0, layer_id] for layer_id in range(layers)]
        acc_second = [acc_out[0, 0, layer_id] for layer_id in range(layers)]
        dx_all = jnp.zeros((stages,) + dy_in.shape[1:], jnp.bfloat16)
        loop_state = lax.fori_loop(0, stages - 1, loop_body, (dy_in[0], acc_first, acc_second, dx_all))
        final_state = run_step(stages - 1, loop_state)
        sum_first = lax.psum(jnp.stack(final_state[1]).astype(jnp.bfloat16), 'dp')
        sum_second = lax.psum(jnp.stack(final_state[2]).astype(jnp.bfloat16), 'dp')
        grad_in = (sum_first.astype(jnp.float32) / replicas)[None]
        grad_out = (sum_second.astype(jnp.float32) / replicas)[None]
        from_first = jnp.where(stage_id == 0, final_state[3], jnp.zeros_like(final_state[3]))
        dx_out = lax.psum_scatter(from_first, 'pp', scatter_dimension=0, tiled=True)
        return grad_in, grad_out, dx_out

    return jax.shard_map(device_fn, mesh=mesh, in_specs=(P('pp'), P('pp'), P('pp', None, None, 'dp'), P('pp', None, None, 'dp'), P('pp', 'dp'), P('pp', 'dp'), P('pp', 'dp')), out_specs=(P('pp'), P('pp'), P('pp', 'dp')), check_vma=False)
```

profile of v0, /device:TPU:0, one launch (start us, length us, event | category | flops | bytes accessed | tf_op | source)
XLA Modules:
  0.0 551.9 jit_solution(4987895799241131684)
XLA Ops:
  8.1 14.2 %slice_bitcast_fusion.2 = (f32[768,3072]{1,0:T(8,128)}, f32[768,3072]{1,0:T(8,128)}) fusion(f32[1,1,2,768,3072]{4,3,2,1,0:T(8,128)} %param.18), kind=kLoop, calls=%fused_computation.166 | loop fusion | bytes 37748736 | tf_op jit(solution)/shard_map/squeeze | solution.py:56
  26.3 7.0 %slice_bitcast_fusion = (f32[3072,768]{1,0:T(8,128)}, f32[3072,768]{1,0:T(8,128)}) fusion(f32[1,1,2,3072,768]{4,3,2,1,0:T(8,128)S(1)} %bitcast.172), kind=kLoop, calls=%fused_computation.164 | loop fusion | bytes 37748736 | tf_op jit(solution)/shard_map/squeeze | solution.py:57
  33.4 159.1 %while.23 = (s32[]{:T(128)}, bf16[64,768]{1,0:T(8,128)(2,1)S(1)}, f32[768,3072]{1,0:T(8,128)}, f32[768,3072]{1,0:T(8,128)}, f32[3072,768]{1,0:T(8,128)}, /*index...) while((s32[]{:T(128)}, bf16[64,768]{1,0:T(8,128)(2,1)S(1)}, ...), condition=%wide.region_3.4_spmd, body=%wide.region_0.3_spmd.sunk | while | flops 2437840896 | bytes 336200512 | solution.py:59
  33.4 46.1 %conditional.4 = (bf16[64,768]{1,0:T(8,128)(2,1)}, f32[768,3072]{1,0:T(8,128)}, f32[768,3072]{1,0:T(8,128)}, f32[3072,768]{1,0:T(8,128)}, f32[3072,768]{1,0:T(8,128)}, /*index=5*/bf16[1,64,768]{2,1,0:T(8,128)(2,1)S(1)}) conditional(s32[]{:T(128)} %convert_element_type.122, (bf16[64,768]{1,0:T(8,128)(2,1)S(1)}, f32[768,3072]{1,0:T(8,128)}, ...), branch_computations={%region_1.0_spmd, %region_2.2_spmd} | conditional | flops 2437840896 | bytes 335413760 | solution.py:47
  37.7 4.7 fusion.21
  48.1 12.3 %convolution_add_fusion.1 = f32[3072,768]{1,0:T(8,128)} fusion(f32[3072,768]{1,0:T(8,128)} %get-tuple-element.311, bf16[64,768]{1,0:T(8,128)(2,1)S(1)} %fusion.21, bf16[4,2,64,3072]{3,2,1,0:T(8,128)(2,1)} %get-tuple-element.305, s32[]{:T(128)S(6)} %select_n.20), kind=kOutput, calls=%fused_computation.1 | convolution fusion | flops 306315264 | bytes 19365892 | tf_op jit(solution)/shard_map/while/body/eval_jaxpr/cond/branch_1_fun/dot_general | solution.py:14
  63.4 7.9 %fusion.18 = bf16[64,768]{1,0:T(8,128)(2,1)} fusion(bf16[64,3072]{1,0:T(8,128)(2,1)S(1)} %fusion.28, bf16[2,768,3072]{2,1,0:T(8,128)(2,1)} %get-tuple-element.307, bf16[64,768]{1,0:T(8,128)(2,1)S(1)} %fusion.21), kind=kOutput, calls=%fused_computation.28 | convolution fusion | flops 302137344 | bytes 5308416 | tf_op jit(solution)/shard_map/while/body/eval_jaxpr/cond/branch_1_fun/dot_general | solution.py:15
  80.8 6.5 %collective-permute-done = bf16[64,768]{1,0:T(8,128)(2,1)S(1)} collective-permute-done((bf16[64,768]{1,0:T(8,128)(2,1)}, bf16[64,768]{1,0:T(8,128)(2,1)S(1)}, u32[]{:S(2)}, u32[]{:S(2)}) %collective-permute-start) | collective-permute-done | bytes 98336 | tf_op jit(solution)/shard_map/while/body/eval_jaxpr/ppermute | solution.py:53
  87.3 46.1 %conditional.4 = (bf16[64,768]{1,0:T(8,128)(2,1)}, f32[768,3072]{1,0:T(8,128)}, f32[768,3072]{1,0:T(8,128)}, f32[3072,768]{1,0:T(8,128)}, f32[3072,768]{1,0:T(8,128)}, /*index=5*/bf16[1,64,768]{2,1,0:T(8,128)(2,1)S(1)}) conditional(s32[]{:T(128)} %convert_element_type.122, (bf16[64,768]{1,0:T(8,128)(2,1)S(1)}, f32[768,3072]{1,0:T(8,128)}, ...), branch_computations={%region_1.0_spmd, %region_2.2_spmd} | conditional | flops 2437840896 | bytes 335413760 | solution.py:47
  91.5 4.7 fusion.21
  102.0 12.3 %convolution_add_fusion.1 = f32[3072,768]{1,0:T(8,128)} fusion(f32[3072,768]{1,0:T(8,128)} %get-tuple-element.311, bf16[64,768]{1,0:T(8,128)(2,1)S(1)} %fusion.21, bf16[4,2,64,3072]{3,2,1,0:T(8,128)(2,1)} %get-tuple-element.305, s32[]{:T(128)S(6)} %select_n.20), kind=kOutput, calls=%fused_computation.1 | convolution fusion | flops 306315264 | bytes 19365892 | tf_op jit(solution)/shard_map/while/body/eval_jaxpr/cond/branch_1_fun/dot_general | solution.py:14
  117.3 7.9 %fusion.18 = bf16[64,768]{1,0:T(8,128)(2,1)} fusion(bf16[64,3072]{1,0:T(8,128)(2,1)S(1)} %fusion.28, bf16[2,768,3072]{2,1,0:T(8,128)(2,1)} %get-tuple-element.307, bf16[64,768]{1,0:T(8,128)(2,1)S(1)} %fusion.21), kind=kOutput, calls=%fused_computation.28 | convolution fusion | flops 302137344 | bytes 5308416 | tf_op jit(solution)/shard_map/while/body/eval_jaxpr/cond/branch_1_fun/dot_general | solution.py:15
  134.7 5.2 collective-permute-done
  139.9 46.1 %conditional.4 = (bf16[64,768]{1,0:T(8,128)(2,1)}, f32[768,3072]{1,0:T(8,128)}, f32[768,3072]{1,0:T(8,128)}, f32[3072,768]{1,0:T(8,128)}, f32[3072,768]{1,0:T(8,128)}, /*index=5*/bf16[1,64,768]{2,1,0:T(8,128)(2,1)S(1)}) conditional(s32[]{:T(128)} %convert_element_type.122, (bf16[64,768]{1,0:T(8,128)(2,1)S(1)}, f32[768,3072]{1,0:T(8,128)}, ...), branch_computations={%region_1.0_spmd, %region_2.2_spmd} | conditional | flops 2437840896 | bytes 335413760 | solution.py:47
  144.1 4.7 fusion.21
  154.6 12.3 %convolution_add_fusion.1 = f32[3072,768]{1,0:T(8,128)} fusion(f32[3072,768]{1,0:T(8,128)} %get-tuple-element.311, bf16[64,768]{1,0:T(8,128)(2,1)S(1)} %fusion.21, bf16[4,2,64,3072]{3,2,1,0:T(8,128)(2,1)} %get-tuple-element.305, s32[]{:T(128)S(6)} %select_n.20), kind=kOutput, calls=%fused_computation.1 | convolution fusion | flops 306315264 | bytes 19365892 | tf_op jit(solution)/shard_map/while/body/eval_jaxpr/cond/branch_1_fun/dot_general | solution.py:14
  169.9 7.9 %fusion.18 = bf16[64,768]{1,0:T(8,128)(2,1)} fusion(bf16[64,3072]{1,0:T(8,128)(2,1)S(1)} %fusion.28, bf16[2,768,3072]{2,1,0:T(8,128)(2,1)} %get-tuple-element.307, bf16[64,768]{1,0:T(8,128)(2,1)S(1)} %fusion.21), kind=kOutput, calls=%fused_computation.28 | convolution fusion | flops 302137344 | bytes 5308416 | tf_op jit(solution)/shard_map/while/body/eval_jaxpr/cond/branch_1_fun/dot_general | solution.py:15
  187.3 5.2 collective-permute-done
  192.5 72.7 %conditional.2 = (bf16[1,3072,768]{2,1,0:T(8,128)(2,1)}, bf16[1,3072,768]{2,1,0:T(8,128)(2,1)}, bf16[1,64,768]{2,1,0:T(8,128)(2,1)S(1)}, bf16[1,768,3072]{2,1,0:T(8,128)(2,1)}, bf16[1,768,3072]{2,1,0:T(8,128)(2,1)}) conditional(s32[]{:T(128)} %convert_element_type.90, (bf16[64,768]{1,0:T(8,128)(2,1)S(1)}, f32[768,3072]{1,0:T(8,128)}, ...), branch_computations={%region_4.5_spmd, %region_5.6_spmd} | conditional | flops 2447278080 | bytes 231407840 | solution.py:47
  196.7 4.7 fusion.97
  210.5 9.5 %copy.12 = f32[768,3072]{0,1:T(8,128)} copy(f32[768,3072]{1,0:T(8,128)} %get-tuple-element.391) | data formatting | bytes 18874368 | tf_op jit(solution)/shard_map
  220.0 7.4 %fusion.86 = bf16[1,768,3072]{1,2,0:T(8,128)(2,1)} fusion(f32[768,3072]{0,1:T(8,128)} %copy.12, bf16[64,3072]{1,0:T(8,128)(2,1)S(1)} %fusion.107, bf16[4,2,64,768]{3,2,1,0:T(8,128)(2,1)} %get-tuple-element.336), kind=kOutput, calls=%fused_computation.99 | convolution fusion | flops 306708480 | bytes 14647296 | tf_op jit(solution)/shard_map/cond/branch_1_fun/dot_general | solution.py:13
  227.5 6.6 %copy.17 = bf16[1,768,3072]{2,1,0:T(8,128)(2,1)} copy(bf16[1,768,3072]{1,2,0:T(8,128)(2,1)} %fusion.86) | data formatting | bytes 9437184 | tf_op jit(solution)/shard_map/cond
  234.1 7.5 %fusion.84 = bf16[1,3072,768]{2,1,0:T(8,128)(2,1)} fusion(f32[3072,768]{1,0:T(8,128)} %get-tuple-element.338, bf16[64,768]{1,0:T(8,128)(2,1)S(1)} %fusion.97, bf16[4,2,64,3072]{3,2,1,0:T(8,128)(2,1)} %get-tuple-element.333), kind=kOutput, calls=%fused_computation.97 | convolution fusion | flops 308674560 | bytes 14647296 | tf_op jit(solution)/shard_map/cond/branch_1_fun/dot_general | solution.py:14
  241.6 9.5 %copy.13 = f32[768,3072]{0,1:T(8,128)} copy(f32[768,3072]{1,0:T(8,128)} %get-tuple-element.392) | data formatting | bytes 18874368 | tf_op jit(solution)/shard_map
  251.1 7.4 %fusion.87 = bf16[1,768,3072]{1,2,0:T(8,128)(2,1)} fusion(f32[768,3072]{0,1:T(8,128)} %copy.13, bf16[64,3072]{1,0:T(8,128)(2,1)S(1)} %fusion.110, bf16[4,2,64,768]{3,2,1,0:T(8,128)(2,1)} %get-tuple-element.336), kind=kOutput, calls=%fused_computation.100 | convolution fusion | flops 306708480 | bytes 14647296 | tf_op jit(solution)/shard_map/cond/branch_1_fun/dot_general | solution.py:13
  258.5 6.6 %copy.19 = bf16[1,768,3072]{2,1,0:T(8,128)(2,1)} copy(bf16[1,768,3072]{1,2,0:T(8,128)(2,1)} %fusion.87) | data formatting | bytes 9437184 | tf_op jit(solution)/shard_map/cond
  265.2 8.4 %pad_maximum_fusion.1 = bf16[2,3072,768]{2,1,0:T(8,128)(2,1)} fusion(bf16[1,3072,768]{2,1,0:T(8,128)(2,1)} %get-tuple-element.379, bf16[1,3072,768]{2,1,0:T(8,128)(2,1)} %get-tuple-element.378), kind=kLoop, calls=%fused_computation.163 | loop fusion | flops 4718592 | bytes 18874368 | tf_op jit(solution)/shard_map/stack | solution.py:62
  273.5 8.4 %pad_maximum_fusion = bf16[2,768,3072]{2,1,0:T(8,128)(2,1)} fusion(bf16[1,768,3072]{2,1,0:T(8,128)(2,1)} %get-tuple-element.396, bf16[1,768,3072]{2,1,0:T(8,128)(2,1)} %get-tuple-element.395), kind=kLoop, calls=%fused_computation.162 | loop fusion | flops 4718592 | bytes 18874368 | tf_op jit(solution)/shard_map/stack | solution.py:61
  282.8 236.4 %all-reduce.3.cloned.1.call-done = (bf16[2,768,3072]{2,1,0:T(8,128)(2,1)}, bf16[2,3072,768]{2,1,0:T(8,128)(2,1)}) async-done(((bf16[2,768,3072]{2,1,0:T(8,128)(2,1)}, bf16[2,3072,768]{2,1,0:T(8,128)(2,1)}), (bf16[2,768,3072]{2,1,0:T(8,128)(2,1)}, bf16[2,3072,768]{2,1,0:T(8,128)(2,1)})) %all-reduce.3.cloned.1.call-update) | async-done | bytes 18874384 | tf_op jit(solution)/shard_map/psum | solution.py:61
  519.2 12.0 %multiply_bitcast_fusion = f32[1,2,3072,768]{3,2,1,0:T(8,128)} fusion(bf16[2,3072,768]{2,1,0:T(8,128)(2,1)} %get-tuple-element.422), kind=kLoop, calls=%fused_computation.160 | loop fusion | flops 9437184 | bytes 28311552 | tf_op jit(solution)/shard_map/broadcast_in_dim | solution.py:64
  531.2 13.2 %multiply_bitcast_fusion.1 = f32[1,2,768,3072]{3,2,1,0:T(8,128)} fusion(bf16[2,768,3072]{2,1,0:T(8,128)(2,1)} %get-tuple-element.421), kind=kLoop, calls=%fused_computation.161 | loop fusion | flops 9437184 | bytes 28311552 | tf_op jit(solution)/shard_map/broadcast_in_dim | solution.py:63
  (155 shorter events, 84.8 us)
Async XLA Ops:
  8.0 511.2 %all-reduce.3.cloned.1.call-start = ((), (), s32[]{:S(2)}) async-start(), calls=%async_computation.2 | async-start | bytes 37748736 | tf_op jit(solution)/shard_map/psum | solution.py:61
  8.0 14.3 %slice-start.12 = ((s8[18874368]{0:T(1024)(128)(4,1)}), s8[2097152]{0:T(1024)(128)(4,1)S(1)}, s32[]{:S(2)}) async-start(s8[18874368]{0:T(1024)(128)(4,1)} %bitcast.171), calls=%async_computation.15 | async-start | bytes 4194304
  8.1 14.3 %slice-start.13 = ((s8[18874368]{0:T(1024)(128)(4,1)}), s8[4194304]{0:T(1024)(128)(4,1)S(1)}, s32[]{:S(2)}) async-start(s8[18874368]{0:T(1024)(128)(4,1)} %bitcast.171), calls=%async_computation.16 | async-start | bytes 8388608
  8.1 15.9 %slice-start.14 = ((s8[18874368]{0:T(1024)(128)(4,1)}), s8[4194304]{0:T(1024)(128)(4,1)S(1)}, s32[]{:S(2)}) async-start(s8[18874368]{0:T(1024)(128)(4,1)} %bitcast.171), calls=%async_computation.17 | async-start | bytes 8388608
  8.1 17.1 %slice-start.15 = ((s8[18874368]{0:T(1024)(128)(4,1)}), s8[4194304]{0:T(1024)(128)(4,1)S(1)}, s32[]{:S(2)}) async-start(s8[18874368]{0:T(1024)(128)(4,1)} %bitcast.171), calls=%async_computation.18 | async-start | bytes 8388608
  8.1 18.2 %slice-start.16 = ((s8[18874368]{0:T(1024)(128)(4,1)}), s8[4194304]{0:T(1024)(128)(4,1)S(1)}, s32[]{:S(2)}) async-start(s8[18874368]{0:T(1024)(128)(4,1)} %bitcast.171), calls=%async_computation.19 | async-start | bytes 8388608
  33.4 11.7 %slice-start.9 = ((s8[9437184]{0:T(1024)(128)(4,1)}), s8[4194304]{0:T(1024)(128)(4,1)S(1)}, s32[]{:S(2)}) async-start(s8[9437184]{0:T(1024)(128)(4,1)} %bitcast.166), calls=%async_computation.12 | async-start | bytes 8388608 | tf_op jit(solution)/shard_map/while/body/eval_jaxpr/cond
  45.2 15.3 %slice-start.6 = ((s8[9437184]{0:T(1024)(128)(4,1)}), s8[4194304]{0:T(1024)(128)(4,1)S(1)}, s32[]{:S(2)}) async-start(s8[9437184]{0:T(1024)(128)(4,1)} %bitcast.164), calls=%async_computation.9 | async-start | bytes 8388608 | tf_op jit(solution)/shard_map/while/body/eval_jaxpr/cond
  45.2 15.3 %slice-start.7 = ((s8[9437184]{0:T(1024)(128)(4,1)}), s8[4194304]{0:T(1024)(128)(4,1)S(1)}, s32[]{:S(2)}) async-start(s8[9437184]{0:T(1024)(128)(4,1)} %bitcast.164), calls=%async_computation.10 | async-start | bytes 8388608 | tf_op jit(solution)/shard_map/while/body/eval_jaxpr/cond
  48.1 12.4 %copy-start.2 = (f32[768,3072]{1,0:T(8,128)}, f32[768,3072]{1,0:T(8,128)S(1)}, u32[]{:S(2)}) copy-start(f32[768,3072]{1,0:T(8,128)S(1)} %convolution_add_fusion.3) | copy-start | bytes 28311556 | tf_op jit(solution)/shard_map/while/body/eval_jaxpr/cond
  48.1 12.4 %slice-start.8 = ((s8[9437184]{0:T(1024)(128)(4,1)}), s8[1048576]{0:T(1024)(128)(4,1)S(1)}, s32[]{:S(2)}) async-start(s8[9437184]{0:T(1024)(128)(4,1)} %bitcast.164), calls=%async_computation.11 | async-start | bytes 2097152 | tf_op jit(solution)/shard_map/while/body/eval_jaxpr/cond
  63.4 12.4 %copy-start.1 = (f32[768,3072]{1,0:T(8,128)}, f32[768,3072]{1,0:T(8,128)S(1)}, u32[]{:S(2)}) copy-start(f32[768,3072]{1,0:T(8,128)S(1)} %convolution_add_fusion.2) | copy-start | bytes 28311556 | tf_op jit(solution)/shard_map/while/body/eval_jaxpr/cond
  79.5 7.8 %collective-permute-start = (bf16[64,768]{1,0:T(8,128)(2,1)}, bf16[64,768]{1,0:T(8,128)(2,1)S(1)}, u32[]{:S(2)}, u32[]{:S(2)}) collective-permute-start(bf16[64,768]{1,0:T(8,128)(2,1)} %get-tuple-element.508), channel_id=1, source_target_pairs={{8,0},{16,8},{24,16},{9,1},{17,9},{25,17},{10,2},{18,10},{26,18},{... | collective-permute-start | bytes 294920 | tf_op jit(solution)/shard_map/while/body/eval_jaxpr/ppermute | solution.py:53
  87.3 11.7 %slice-start.9 = ((s8[9437184]{0:T(1024)(128)(4,1)}), s8[4194304]{0:T(1024)(128)(4,1)S(1)}, s32[]{:S(2)}) async-start(s8[9437184]{0:T(1024)(128)(4,1)} %bitcast.166), calls=%async_computation.12 | async-start | bytes 8388608 | tf_op jit(solution)/shard_map/while/body/eval_jaxpr/cond
  87.3 11.7 %slice-start.10 = ((s8[9437184]{0:T(1024)(128)(4,1)}), s8[4194304]{0:T(1024)(128)(4,1)S(1)}, s32[]{:S(2)}) async-start(s8[9437184]{0:T(1024)(128)(4,1)} %bitcast.166), calls=%async_computation.13 | async-start | bytes 8388608 | tf_op jit(solution)/shard_map/while/body/eval_jaxpr/cond
  99.0 15.3 %slice-start.6 = ((s8[9437184]{0:T(1024)(128)(4,1)}), s8[4194304]{0:T(1024)(128)(4,1)S(1)}, s32[]{:S(2)}) async-start(s8[9437184]{0:T(1024)(128)(4,1)} %bitcast.164), calls=%async_computation.9 | async-start | bytes 8388608 | tf_op jit(solution)/shard_map/while/body/eval_jaxpr/cond
  99.1 15.3 %slice-start.7 = ((s8[9437184]{0:T(1024)(128)(4,1)}), s8[4194304]{0:T(1024)(128)(4,1)S(1)}, s32[]{:S(2)}) async-start(s8[9437184]{0:T(1024)(128)(4,1)} %bitcast.164), calls=%async_computation.10 | async-start | bytes 8388608 | tf_op jit(solution)/shard_map/while/body/eval_jaxpr/cond
  102.0 12.4 %copy-start.2 = (f32[768,3072]{1,0:T(8,128)}, f32[768,3072]{1,0:T(8,128)S(1)}, u32[]{:S(2)}) copy-start(f32[768,3072]{1,0:T(8,128)S(1)} %convolution_add_fusion.3) | copy-start | bytes 28311556 | tf_op jit(solution)/shard_map/while/body/eval_jaxpr/cond
  102.0 12.4 %slice-start.8 = ((s8[9437184]{0:T(1024)(128)(4,1)}), s8[1048576]{0:T(1024)(128)(4,1)S(1)}, s32[]{:S(2)}) async-start(s8[9437184]{0:T(1024)(128)(4,1)} %bitcast.164), calls=%async_computation.11 | async-start | bytes 2097152 | tf_op jit(solution)/shard_map/while/body/eval_jaxpr/cond
  117.3 12.4 %copy-start.1 = (f32[768,3072]{1,0:T(8,128)}, f32[768,3072]{1,0:T(8,128)S(1)}, u32[]{:S(2)}) copy-start(f32[768,3072]{1,0:T(8,128)S(1)} %convolution_add_fusion.2) | copy-start | bytes 28311556 | tf_op jit(solution)/shard_map/while/body/eval_jaxpr/cond
  133.4 6.5 %collective-permute-start = (bf16[64,768]{1,0:T(8,128)(2,1)}, bf16[64,768]{1,0:T(8,128)(2,1)S(1)}, u32[]{:S(2)}, u32[]{:S(2)}) collective-permute-start(bf16[64,768]{1,0:T(8,128)(2,1)} %get-tuple-element.508), channel_id=1, source_target_pairs={{8,0},{16,8},{24,16},{9,1},{17,9},{25,17},{10,2},{18,10},{26,18},{... | collective-permute-start | bytes 294920 | tf_op jit(solution)/shard_map/while/body/eval_jaxpr/ppermute | solution.py:53
  139.9 11.7 %slice-start.9 = ((s8[9437184]{0:T(1024)(128)(4,1)}), s8[4194304]{0:T(1024)(128)(4,1)S(1)}, s32[]{:S(2)}) async-start(s8[9437184]{0:T(1024)(128)(4,1)} %bitcast.166), calls=%async_computation.12 | async-start | bytes 8388608 | tf_op jit(solution)/shard_map/while/body/eval_jaxpr/cond
  139.9 11.7 %slice-start.10 = ((s8[9437184]{0:T(1024)(128)(4,1)}), s8[4194304]{0:T(1024)(128)(4,1)S(1)}, s32[]{:S(2)}) async-start(s8[9437184]{0:T(1024)(128)(4,1)} %bitcast.166), calls=%async_computation.13 | async-start | bytes 8388608 | tf_op jit(solution)/shard_map/while/body/eval_jaxpr/cond
  151.6 15.3 %slice-start.6 = ((s8[9437184]{0:T(1024)(128)(4,1)}), s8[4194304]{0:T(1024)(128)(4,1)S(1)}, s32[]{:S(2)}) async-start(s8[9437184]{0:T(1024)(128)(4,1)} %bitcast.164), calls=%async_computation.9 | async-start | bytes 8388608 | tf_op jit(solution)/shard_map/while/body/eval_jaxpr/cond
  151.7 15.3 %slice-start.7 = ((s8[9437184]{0:T(1024)(128)(4,1)}), s8[4194304]{0:T(1024)(128)(4,1)S(1)}, s32[]{:S(2)}) async-start(s8[9437184]{0:T(1024)(128)(4,1)} %bitcast.164), calls=%async_computation.10 | async-start | bytes 8388608 | tf_op jit(solution)/shard_map/while/body/eval_jaxpr/cond
  154.6 12.4 %copy-start.2 = (f32[768,3072]{1,0:T(8,128)}, f32[768,3072]{1,0:T(8,128)S(1)}, u32[]{:S(2)}) copy-start(f32[768,3072]{1,0:T(8,128)S(1)} %convolution_add_fusion.3) | copy-start | bytes 28311556 | tf_op jit(solution)/shard_map/while/body/eval_jaxpr/cond
  154.6 12.4 %slice-start.8 = ((s8[9437184]{0:T(1024)(128)(4,1)}), s8[1048576]{0:T(1024)(128)(4,1)S(1)}, s32[]{:S(2)}) async-start(s8[9437184]{0:T(1024)(128)(4,1)} %bitcast.164), calls=%async_computation.11 | async-start | bytes 2097152 | tf_op jit(solution)/shard_map/while/body/eval_jaxpr/cond
  169.9 12.4 %copy-start.1 = (f32[768,3072]{1,0:T(8,128)}, f32[768,3072]{1,0:T(8,128)S(1)}, u32[]{:S(2)}) copy-start(f32[768,3072]{1,0:T(8,128)S(1)} %convolution_add_fusion.2) | copy-start | bytes 28311556 | tf_op jit(solution)/shard_map/while/body/eval_jaxpr/cond
  186.0 6.5 %collective-permute-start = (bf16[64,768]{1,0:T(8,128)(2,1)}, bf16[64,768]{1,0:T(8,128)(2,1)S(1)}, u32[]{:S(2)}, u32[]{:S(2)}) collective-permute-start(bf16[64,768]{1,0:T(8,128)(2,1)} %get-tuple-element.508), channel_id=1, source_target_pairs={{8,0},{16,8},{24,16},{9,1},{17,9},{25,17},{10,2},{18,10},{26,18},{... | collective-permute-start | bytes 294920 | tf_op jit(solution)/shard_map/while/body/eval_jaxpr/ppermute | solution.py:53
  192.5 11.7 %slice-start.3 = ((s8[9437184]{0:T(1024)(128)(4,1)}), s8[4194304]{0:T(1024)(128)(4,1)S(1)}, s32[]{:S(2)}) async-start(s8[9437184]{0:T(1024)(128)(4,1)} %bitcast.162), calls=%async_computation.6 | async-start | bytes 8388608 | tf_op jit(solution)/shard_map/cond
  192.5 11.8 %slice-start.4 = ((s8[9437184]{0:T(1024)(128)(4,1)}), s8[4194304]{0:T(1024)(128)(4,1)S(1)}, s32[]{:S(2)}) async-start(s8[9437184]{0:T(1024)(128)(4,1)} %bitcast.162), calls=%async_computation.7 | async-start | bytes 8388608 | tf_op jit(solution)/shard_map/cond
  281.9 262.5 %reduce-scatter.2.cloned.1.call-start = ((), (), s32[]{:S(2)}) async-start(), calls=%async_computation.1 | async-start | bytes 491520 | tf_op jit(solution)/shard_map/reduce_scatter | solution.py:66
  (25 other events, 194.4 us)
Sparse Core Ops, SparseCore 0:
  282.1 237.0 all-reduce.2
Sparse Core Ops, SparseCore 1:
  285.3 19.2 reduce-scatter.1
where the time goes:
time: 553 us; the launch traced here: 552 us
  waiting for transfers between devices  253 us (46%)
  matrix products  167 us (30%)
  local copies, waits for them, and re-layouts  68.8 us (12%)
  other arithmetic  42.8 us (8%)
  between operations  15.6 us (3%)
    psum x1, waiting for transfers between devices, device_fn(): sum_first = lax.psum(jnp.stack(final_state[1]).astype(jnp.bfloat16), 'dp')  236 us
    dot_general x8, matrix products, layer_backward(): lax.dot_general(act_bf, cot_in, (((0,), (0,)), ((), ())), preferred_eleme...  62.5 us
    dot_general x8, matrix products, layer_backward(): lax.dot_general(d_pre, w_first, (((1,), (1,)), ((), ())), preferred_eleme...  44.2 us
    dot_general x8, matrix products, layer_backward(): lax.dot_general(x_in, d_pre, (((0,), (0,)), ((), ())), preferred_element_...  32.1 us
    dot_general x8, matrix products, layer_backward(): lax.dot_general(cot_in, w_second, (((1,), (1,)), ((), ())), preferred_ele...  27.8 us
    cond x97, local copies, waits for them, and re-layouts  24.4 us
    another operation x3, local copies, waits for them, and re-layouts  19.1 us
    ppermute x3, waiting for transfers between devices, loop_body(): cot_next = lax.ppermute(cot_cur, 'pp', perm=down_pairs)  16.8 us
  transfers between devices with their start and end apart: 5, of which 4 were waited for; matrix products, arithmetic and copies ran while one was open for 5% of the time, Pallas kernels for 0%

commit v1 on v0

v1 whole, which is shorter than its diff:
```python
import functools
import jax
import jax.numpy as jnp
from jax import lax
from jax.experimental import pallas as pl
from jax.experimental.pallas import tpu as pltpu
from jax.sharding import PartitionSpec as P

BF16 = jnp.bfloat16
F32 = jnp.float32
NT = (((1,), (1,)), ((), ()))
COLS = 2
RING = 4


def gelu_and_slope(h):
    root = 0.7978845608028654
    cube = 0.044715
    sq = h * h
    th = jnp.tanh(root * (h + cube * (h * sq)))
    cdf = 0.5 * (1.0 + th)
    slope = cdf + (0.5 * root) * h * (1.0 - th * th) * (1.0 + (3.0 * cube) * sq)
    return h * cdf, slope


def main_kernel(sizes, w_in, w_out, x_saved, h_saved, dy_in, acc_in, acc_out,
                m_ref, dx_ref,
                wi_s, wo_s, lt_s, rm_s, xs_s, cb_s, acc_s, p_s, h1_s, h2_s,
                wsem, hsem, xsem, dysem, accsem, cot_send, cot_recv, dx_send, dx_recv, dx_loc,
                send_sem, recv_sem, free_sem):
    hid, ff, tok, stages = sizes
    cw = hid // COLS
    nq = ff // cw
    per_kind = nq
    per_layer = 2 * nq
    total = 2 * per_layer
    nblk = ff // hid
    unit = hid // 16
    rows4 = stages * tok

    pp = lax.axis_index('pp')
    dp = lax.axis_index('dp')
    core = dp % 2
    xc = (dp // 2) % 2
    yc = dp // 4
    pair = dp + 1 - 2 * core
    xn = dp + 2 - 4 * xc
    yn = dp + 4 - 8 * yc

    def dev(pp_i, dp_i):
        return dict(device_id=(pp_i, dp_i), device_id_type=pl.DeviceIdType.MESH)

    def w_copy(k, which):
        if which == 0:
            return [pltpu.make_async_copy(w_out.at[0, k], wo_s.at[k], wsem.at[k, 0])]
        return [pltpu.make_async_copy(w_in.at[0, k, :, pl.ds(q * cw, cw)], wi_s.at[k, q], wsem.at[k, 1 + q]) for q in range(nq)]

    def h_copy(k, t, q):
        return pltpu.make_async_copy(h_saved.at[0, t, k, :, pl.ds(pl.multiple_of(q * cw, 128), cw)],
                                     rm_s.at[k, COLS + q, pl.ds(pl.multiple_of(t * tok, tok), tok), :], hsem.at[k, t, q])

    def x_copy():
        return pltpu.make_async_copy(x_saved.at[0], xs_s, xsem)

    dy_copy = pltpu.make_async_copy(dy_in.at[0], cb_s.at[0], dysem)

    def acc_where(c):
        k = 1 - c // per_layer
        b = c % per_layer
        return k, b // per_kind, b % per_kind

    def acc_copies(c):
        k, kind, jj = acc_where(c)
        slot = c % 2
        a = pltpu.make_async_copy(acc_out.at[0, 0, k, pl.ds(pl.multiple_of((jj // COLS) * hid, 128), hid), pl.ds(pl.multiple_of((jj % COLS) * cw, 128), cw)],
                                  acc_s.at[slot], accsem.at[slot])
        b = pltpu.make_async_copy(acc_in.at[0, 0, k, :, pl.ds(pl.multiple_of(jj * cw, 128), cw)], acc_s.at[slot], accsem.at[slot])
        return kind, a, b

    def acc_start(c):
        kind, a, b = acc_copies(c)

        @pl.when(kind == 0)
        def _():
            a.start()

        @pl.when(kind == 1)
        def _():
            b.start()

    def acc_wait(c):
        acc_copies(c)[2].wait()

    dy_copy.start()
    for k in (1, 0):
        for q in range(nq):
            h_copy(k, 0, q).start()
        for which in (0, 1):
            for cp in w_copy(k, which):
                cp.start()
    x_copy().start()

    def h_rest(i, carry):
        k = 1 - i % 2
        t = 1 + i // 2
        for q in range(nq):
            h_copy(k, t, q).start()
        return carry

    lax.fori_loop(0, 2 * (stages - 1), h_rest, 0)
    acc_start(0)

    barrier = pltpu.get_barrier_semaphore()
    for other in (pair, xn, yn):
        pl.semaphore_signal(barrier, inc=1, **dev(pp, other))
    for step in range(1, stages):
        pl.semaphore_signal(barrier, inc=1, **dev((pp + step) % stages, dp))
    pl.semaphore_wait(barrier, 3 + stages - 1)

    def cot_copy(t):
        return pltpu.make_async_remote_copy(src_ref=cb_s.at[t], dst_ref=cb_s.at[t + 1], send_sem=cot_send.at[t], recv_sem=cot_recv.at[t + 1],
                                            **dev(jnp.maximum(pp - 1, 0), dp))

    def cot_arrival(t):
        return pltpu.make_async_remote_copy(src_ref=cb_s.at[t], dst_ref=cb_s.at[t], send_sem=cot_send.at[0], recv_sem=cot_recv.at[t],
                                            **dev(jnp.maximum(pp - 1, 0), dp))

    def dx_copy(t):
        return pltpu.make_async_remote_copy(src_ref=cb_s.at[t], dst_ref=dx_ref.at[0], send_sem=dx_send.at[t], recv_sem=dx_recv,
                                            **dev(t, dp))

    def layer(t, k, cot):
        rows = pl.ds(pl.multiple_of(t * tok, tok), tok)
        for j in range(COLS):
            rm_s[k, j, rows, :] = cot[:, j * cw:(j + 1) * cw]
        back = cot.astype(F32)
        for q in range(nq):
            e = lax.dot_general(cot, wo_s[k, q * cw:(q + 1) * cw, :], NT, preferred_element_type=F32)
            _, slope = gelu_and_slope(rm_s[k, COLS + q, rows, :].astype(F32))
            dh = (e * slope).astype(BF16)
            rm_s[k, COLS + q, rows, :] = dh
            back += lax.dot_general(dh, wi_s[k, q], NT, preferred_element_type=F32)
        return back.astype(BF16)

    def prepare(half):
        cols = pl.ds(half * 2 * tok, 2 * tok)

        def one_layer(k, carry):
            xx = jnp.concatenate([xs_s[2 * half, k], xs_s[2 * half + 1, k]], axis=0)
            lt_s[k, 0, :, cols] = xx.T
            return carry

        lax.fori_loop(0, 2, one_layer, 0)

    def chain_step(t, carry):
        active = pp + t < stages

        first = isinstance(t, int)
        if first:
            dy_copy.wait()
        else:
            @pl.when(active)
            def _():
                cot_arrival(t).wait_recv()

        @pl.when(active)
        def _():
            def one(i, cot_idx):
                k = 1 - i

                if first:
                    for which in (0, 1):
                        for cp in w_copy(k, which):
                            cp.wait()
                cot = cb_s[t]
                out = layer(t, k, cot)
                cb_s[t] = out
                return cot_idx
            lax.fori_loop(0, 2, one, 0)

            @pl.when(pp > 0)
            def _():
                cot_copy(t).start()

            if not first:
                @pl.when(pp == 0)
                def _():
                    dx_copy(t).start()

        return carry

    def h_wait(i, carry):
        for q in range(nq):
            h_copy(1 - i % 2, i // 2, q).wait()
        return carry

    def zero_inactive(t, carry):
        @pl.when(pp + t >= stages)
        def _():
            rows = pl.ds(pl.multiple_of(t * tok, tok), tok)
            zero = jnp.zeros((tok, cw), BF16)

            def one_layer(k, c2):
                for j in range(COLS + nq):
                    rm_s[k, j, rows, :] = zero
                return c2
            lax.fori_loop(0, 2, one_layer, 0)
        return carry

    def acts(half):
        def body(i, carry):
            k = 1 - i // nq
            q = i % nq
            cols = pl.ds(half * 2 * tok, 2 * tok)
            hh = rm_s[k, COLS + q, pl.ds(half * 2 * tok, 2 * tok), :].astype(F32)
            act, _ = gelu_and_slope(hh)
            lt_s[k, 1 + q // COLS, pl.ds(pl.multiple_of((q % COLS) * cw, 128), cw), cols] = act.astype(BF16).T
            return carry
        lax.fori_loop(0, 2 * nq, body, 0)

    lax.fori_loop(0, 4, h_wait, 0)
    acts(0)
    chain_step(0, 0)
    lax.fori_loop(4, 2 * stages, h_wait, 0)
    x_copy().wait()
    for half in range(1, stages // 2):
        acts(half)
    for half in range(stages // 2):
        prepare(half)
    lax.fori_loop(1, stages, zero_inactive, 0)
    lax.fori_loop(1, stages, chain_step, 0)

    half = hid // 2
    hb = core * half
    xb = hb
    yb = hb + 4 * unit

    def rows_of(start, n):
        return pl.ds(pl.multiple_of(start, 16), n)

    def remote(kind, c, src, dst, target):
        return pltpu.make_async_remote_copy(src_ref=src, dst_ref=dst, send_sem=send_sem.at[kind, c % RING], recv_sem=recv_sem.at[kind, c], **dev(pp, target))

    def msg(kind, c, arriving=False):
        f = 1 if arriving else 0
        if kind == 0:
            other = m_ref.at[c, rows_of(half - hb, half), :]
            return remote(0, c, other, p_s.at[c], pair)
        if kind == 1:
            return remote(1, c, p_s.at[c, rows_of((1 - xc) * 2 * unit, 2 * unit), :], h1_s.at[c, 0], xn)
        if kind == 2:
            return remote(2, c, p_s.at[c, rows_of(4 * unit + (1 - yc) * 2 * unit, 2 * unit), :], h1_s.at[c, 1], yn)
        if kind == 3:
            return remote(3, c, h1_s.at[c, 0, rows_of((1 - yc) * unit, unit), :], h2_s.at[c, 0], yn)
        if kind == 4:
            return remote(4, c, h1_s.at[c, 1, rows_of((1 - xc) * unit, unit), :], h2_s.at[c, 1], xn)
        if kind == 5:
            y_of = 1 - yc if f else yc
            r = m_ref.at[c, rows_of(xb + xc * 2 * unit + y_of * unit, unit), :]
            return remote(5, c, r, r, yn)
        if kind == 6:
            x_of = 1 - xc if f else xc
            r = m_ref.at[c, rows_of(yb + yc * 2 * unit + x_of * unit, unit), :]
            return remote(6, c, r, r, xn)
        if kind == 7:
            x_of = 1 - xc if f else xc
            r = m_ref.at[c, rows_of(xb + x_of * 2 * unit, 2 * unit), :]
            return remote(7, c, r, r, xn)
        if kind == 8:
            y_of = 1 - yc if f else yc
            r = m_ref.at[c, rows_of(yb + y_of * 2 * unit, 2 * unit), :]
            return remote(8, c, r, r, yn)
        base = half - hb if f else hb
        r = m_ref.at[c, rows_of(base, half), :]
        return remote(9, c, r, r, pair)

    def send(kind, c):
        if kind > 0:
            @pl.when(c >= RING)
            def _():
                msg(kind, c - RING).wait_send()
        msg(kind, c).start()

    def arrive(kind, c):
        msg(kind, c, True).wait_recv()

    def plus(left, right):
        return (left.astype(F32) + right.astype(F32)).astype(BF16)

    def produce(c):
        @pl.when(c + 1 < total)
        def _():
            acc_start(c + 1)
        acc_wait(c)
        k, kind, jj = acc_where(c)
        li = (1 - kind) * (1 + jj // COLS)
        ri = (1 - kind) * (jj % COLS) + kind * (COLS + jj)
        slot = c % 2
        nr = hid // 6 if hid % 768 == 0 else hid // 2
        for i in range(hid // nr):
            r = pl.ds(i * nr, nr)
            g = jnp.dot(lt_s[k, li, r, :], rm_s[k, ri], preferred_element_type=F32)
            m_ref[c, r, :] = (acc_s[slot, r, :] + g).astype(BF16)
        send(0, c)

    def stage1(c):
        arrive(0, c)
        p_s[c] = plus(p_s[c], m_ref[c, rows_of(hb, half), :])
        send(1, c)
        send(2, c)
        msg(0, c).wait_send()
        pl.semaphore_signal(free_sem, inc=1, **dev(pp, pair))

    def stage2(c):
        arrive(1, c)
        h1_s[c, 0] = plus(h1_s[c, 0], p_s[c, rows_of(xc * 2 * unit, 2 * unit), :])
        send(3, c)
        arrive(2, c)
        h1_s[c, 1] = plus(h1_s[c, 1], p_s[c, rows_of(4 * unit + yc * 2 * unit, 2 * unit), :])
        send(4, c)

    def stage3(c):
        arrive(3, c)
        m_ref[c, rows_of(xb + xc * 2 * unit + yc * unit, unit), :] = plus(h1_s[c, 0, rows_of(yc * unit, unit), :], h2_s[c, 0])
        send(5, c)
        arrive(4, c)
        m_ref[c, rows_of(yb + yc * 2 * unit + xc * unit, unit), :] = plus(h1_s[c, 1, rows_of(xc * unit, unit), :], h2_s[c, 1])
        send(6, c)

    def stage4(c):
        arrive(5, c)
        send(7, c)
        arrive(6, c)
        send(8, c)

    def stage5(c):
        arrive(7, c)
        arrive(8, c)
        pl.semaphore_wait(free_sem, 1)
        send(9, c)

    def stage6(c):
        arrive(9, c)

    plan = ((stage6, 9), (stage5, 8), (stage4, 6), (stage3, 5), (stage2, 3), (stage1, 1), (produce, 0))
    depth = max(lag for _, lag in plan)

    def run(i, carry):
        for fn, lag in plan:
            c = i - lag

            @pl.when((c >= 0) & (c < total))
            def _():
                fn(c)
        return carry

    lax.fori_loop(0, total + depth, run, 0)

    def drain(i, carry):
        for kind in range(1, 10):
            msg(kind, total - RING + i).wait_send()
        return carry

    lax.fori_loop(0, RING, drain, 0)

    @pl.when(pp == 0)
    def _():
        own = pltpu.make_async_copy(cb_s.at[0], dx_ref.at[0], dx_loc)
        own.start()
        own.wait()

        def sent(t, carry):
            dx_copy(t).wait_send()
            return carry
        lax.fori_loop(1, stages, sent, 0)

    @pl.when(pp > 0)
    def _():
        dx_copy(0).wait_recv()

        def sent(t, carry):
            cot_copy(t).wait_send()
            return carry
        lax.fori_loop(0, stages - pp, sent, 0)


def write_kernel(sizes, m_ref, gi_ref, go_ref, out_s, out_sem):
    hid, ff, tok, stages = sizes
    cw = hid // COLS
    nq = ff // cw
    per_layer = 2 * nq
    total = 2 * per_layer
    slots = out_s.shape[0]

    def copies(c):
        k = 1 - c // per_layer
        b = c % per_layer
        kind, jj = b // nq, b % nq
        slot = c % slots
        a = pltpu.make_async_copy(out_s.at[slot], go_ref.at[0, k, pl.ds(pl.multiple_of((jj // COLS) * hid, 128), hid), pl.ds(pl.multiple_of((jj % COLS) * cw, 128), cw)], out_sem.at[slot])
        b = pltpu.make_async_copy(out_s.at[slot], gi_ref.at[0, k, :, pl.ds(pl.multiple_of(jj * cw, 128), cw)], out_sem.at[slot])
        return kind, a, b

    def body(c, carry):
        @pl.when(c >= slots)
        def _():
            copies(c - slots)[2].wait()
        slot = c % slots
        nr = hid // 4
        for i in range(4):
            r = pl.ds(i * nr, nr)
            out_s[slot, r, :] = m_ref[c, r, :].astype(F32) * 0.125
        kind, a, b = copies(c)

        @pl.when(kind == 0)
        def _():
            a.start()

        @pl.when(kind == 1)
        def _():
            b.start()
        return carry

    lax.fori_loop(0, total, body, 0)

    def drain(i, carry):
        copies(total - slots + i)[2].wait()
        return carry
    lax.fori_loop(0, slots, drain, 0)


def solution(mesh):
    stages = mesh.shape['pp']

    def device_fn(w_in, w_out, x_saved, h_saved, dy_in, acc_in, acc_out):
        hid, ff = w_in.shape[2:]
        tok = dy_in.shape[1]
        sizes = (hid, ff, tok, stages)
        cw = hid // COLS
        nq = ff // cw
        total = 4 * nq
        unit = hid // 16
        any_spec = pl.BlockSpec(memory_space=pltpu.HBM)
        vm_spec = pl.BlockSpec(memory_space=pltpu.VMEM)
        m_all, dx = pl.pallas_call(
            functools.partial(main_kernel, sizes),
            out_shape=(pltpu.VMEM((total, hid, cw), BF16), jax.ShapeDtypeStruct((1, tok, hid), BF16)),
            in_specs=[any_spec] * 7,
            out_specs=(vm_spec, vm_spec),
            scratch_shapes=[
                pltpu.VMEM((2, nq, hid, cw), BF16),
                pltpu.VMEM((2, ff, hid), BF16),
                pltpu.VMEM((2, 1 + ff // hid, hid, stages * tok), BF16),
                pltpu.VMEM((2, COLS + nq, stages * tok, cw), BF16),
                pltpu.VMEM((stages, 2, tok, hid), BF16),
                pltpu.VMEM((stages, tok, hid), BF16),
                pltpu.VMEM((2, hid, cw), F32),
                pltpu.VMEM((total, hid // 2, cw), BF16),
                pltpu.VMEM((total, 2, 2 * unit, cw), BF16),
                pltpu.VMEM((total, 2, unit, cw), BF16),
                pltpu.SemaphoreType.DMA((2, 1 + nq)),
                pltpu.SemaphoreType.DMA((2, stages, nq)),
                pltpu.SemaphoreType.DMA,
                pltpu.SemaphoreType.DMA,
                pltpu.SemaphoreType.DMA((2,)),
                pltpu.SemaphoreType.DMA((stages,)),
                pltpu.SemaphoreType.DMA((stages,)),
                pltpu.SemaphoreType.DMA((stages,)),
                pltpu.SemaphoreType.DMA,
                pltpu.SemaphoreType.DMA,
                pltpu.SemaphoreType.DMA((10, RING)),
                pltpu.SemaphoreType.DMA((10, total)),
                pltpu.SemaphoreType.REGULAR,
            ],
            compiler_params=pltpu.CompilerParams(collective_id=0, has_side_effects=True, vmem_limit_bytes=46720 * 1024),
            name='chain_reduce',
        )(w_in, w_out, x_saved, h_saved, dy_in, acc_in, acc_out)
        grad_in, grad_out = pl.pallas_call(
            functools.partial(write_kernel, sizes),
            out_shape=(jax.ShapeDtypeStruct((1, 2, hid, ff), F32), jax.ShapeDtypeStruct((1, 2, ff, hid), F32)),
            in_specs=[vm_spec],
            out_specs=(any_spec, any_spec),
            scratch_shapes=[pltpu.VMEM((4, hid, cw), F32), pltpu.SemaphoreType.DMA((4,))],
            compiler_params=pltpu.CompilerParams(vmem_limit_bytes=16 * 1024 * 1024),
            name='write_out',
        )(m_all)
        return grad_in, grad_out, dx

    return jax.shard_map(device_fn, mesh=mesh, in_specs=(P('pp'), P('pp'), P('pp', None, None, 'dp'), P('pp', None, None, 'dp'), P('pp', 'dp'), P('pp', 'dp'), P('pp', 'dp')), out_specs=(P('pp'), P('pp'), P('pp', 'dp')), check_vma=False)
```

time: 553 us -> 233 us (0.42)
  waiting for transfers between devices: 253 us -> 0 us
  Pallas kernels: 0 us -> 231 us
  matrix products: 167 us -> 0 us
  local copies, waits for them, and re-layouts: 68.8 us -> 0.65 us
  other arithmetic: 42.8 us -> 0 us
  between operations: 15.6 us -> 0.66 us
    psum x1 -> x0, waiting for transfers between devices: 236 us -> none  [device_fn(): sum_first = lax.psum(jnp.stack(final_state[1]).astype(jnp.bfloat16), 'dp')]
    pallas_call x0 -> x2, Pallas kernels: none -> 231 us  [the longest x1 219 us: device_fn(): pl.pallas_call(functools.partial(main_kernel, sizes), out_shape=(pltpu.VM...]
    dot_general x32 -> x0, matrix products: 167 us -> none  [the longest x8 62.5 us: layer_backward(): lax.dot_general(act_bf, cot_in, (((0,), (0,)), ((), ())), preferred_eleme...]
    broadcast_in_dim x2 -> x0, other arithmetic: 25.2 us -> none  [the longest x1 13.2 us: device_fn(): grad_in = (sum_first.astype(jnp.float32) / replicas)[None]]
    cond x97 -> x0, local copies, waits for them, and re-layouts: 24.4 us -> none
    squeeze x2 -> x0, local copies, waits for them, and re-layouts: 21.2 us -> none  [the longest x1 14.2 us: device_fn(): acc_first = [acc_in[0, 0, layer_id] for layer_id in range(layers)]]
    another operation x3 -> x0, local copies, waits for them, and re-layouts: 19.1 us -> none
    ppermute x3 -> x0, waiting for transfers between devices: 16.8 us -> none  [loop_body(): cot_next = lax.ppermute(cot_cur, 'pp', perm=down_pairs)]
  transfers between devices with their start and end apart: 5 -> 0, of which waited for: 4 -> 0; matrix products, arithmetic and copies ran while one was open for 5% -> 0% of each run, Pallas kernels for 0% -> 0%
where the time goes in v1:
time: 233 us
  Pallas kernels  231 us (99%)
    pallas_call x1, Pallas kernels, device_fn(): pl.pallas_call(functools.partial(main_kernel, sizes), out_shape=(pltpu.VM...  219 us
    pallas_call x1, Pallas kernels, device_fn(): pl.pallas_call(functools.partial(write_kernel, sizes), out_shape=(jax.Sha...  12.3 us

profile of v1, /device:TPU:0, one launch (start us, length us, event | category | flops | bytes accessed | tf_op | source)
XLA Modules:
  0.0 232.7 jit_solution(13499751709021508951)
XLA Ops:
  0.6 219.2 %chain_reduce.1 = (bf16[32,768,384]{2,1,0:T(8,128)(2,1)S(1)}, bf16[1,64,768]{2,1,0:T(8,128)(2,1)}) custom-call(bf16[1,2,768,3072]{3,2,1,0:T(8,128)(2,1)} %w_in.1, bf16[1,2,3072,768]{3,2,1,0:T(8,128)(2,1)} %w_out.1, bf16[1,4,2,64,768]{4,3,2,1,0:T(8,128)(2,1)} %x_saved.1, bf16[1,4,2,64,3072]{4,3,2,1,0:T(8,128)(2,1)} %h_saved.1, bf16[1,64,768]{2,1,0:T(8,128)(2,1)} %dy_in.1, ...), custom_call_target="tpu_custom_call" | custom-call | tf_op jit(solution)/shard_map/chain_reduce/pallas_call | solution.py:445
  219.8 0.0 copy-start
  219.8 12.3 %write_out.1 = (f32[1,2,768,3072]{3,2,1,0:T(8,128)}, f32[1,2,3072,768]{3,2,1,0:T(8,128)}) custom-call(bf16[32,768,384]{2,1,0:T(8,128)(2,1)S(1)} %get-tuple-element.7.m_ref), custom_call_target="tpu_custom_call" | custom-call | tf_op jit(solution)/shard_map/write_out/pallas_call | solution.py:478
  232.1 0.0 copy-done
  232.1 0.6 copy.11
Async XLA Ops:
  219.8 12.3 %copy-start = (bf16[1,64,768]{2,1,0:T(8,128)(2,1)S(1)}, bf16[1,64,768]{2,1,0:T(8,128)(2,1)}, u32[]{:S(2)}) copy-start(bf16[1,64,768]{2,1,0:T(8,128)(2,1)} %get-tuple-element.16) | copy-start | bytes 294916

commit v2 on v1

--- a/solution.py
+++ b/solution.py
@@ -10,7 +10,10 @@
 F32 = jnp.float32
 NT = (((1,), (1,)), ((), ()))
 COLS = 2
+TILES = 3
 RING = 4
+RECV_RING = 8
+EARLY = 7
 
 
 def gelu_and_slope(h):
@@ -31,11 +34,12 @@
     hid, ff, tok, stages = sizes
     cw = hid // COLS
     nq = ff // cw
+    nb = ff // hid
     per_kind = nq
     per_layer = 2 * nq
     total = 2 * per_layer
-    nblk = ff // hid
     unit = hid // 16
+    tile = hid // TILES
     rows4 = stages * tok
 
     pp = lax.axis_index('pp')
@@ -50,19 +54,37 @@
     def dev(pp_i, dp_i):
         return dict(device_id=(pp_i, dp_i), device_id_type=pl.DeviceIdType.MESH)
 
-    def w_copy(k, which):
-        if which == 0:
-            return [pltpu.make_async_copy(w_out.at[0, k], wo_s.at[k], wsem.at[k, 0])]
-        return [pltpu.make_async_copy(w_in.at[0, k, :, pl.ds(q * cw, cw)], wi_s.at[k, q], wsem.at[k, 1 + q]) for q in range(nq)]
-
-    def h_copy(k, t, q):
-        return pltpu.make_async_copy(h_saved.at[0, t, k, :, pl.ds(pl.multiple_of(q * cw, 128), cw)],
-                                     rm_s.at[k, COLS + q, pl.ds(pl.multiple_of(t * tok, tok), tok), :], hsem.at[k, t, q])
-
-    def x_copy():
-        return pltpu.make_async_copy(x_saved.at[0], xs_s, xsem)
-
-    dy_copy = pltpu.make_async_copy(dy_in.at[0], cb_s.at[0], dysem)
+    def w_out_copy(k):
+        return pltpu.make_async_copy(w_out.at[0, k], wo_s.at[k], wsem.at[k, 0])
+
+    def w_in_start(k):
+        for j in range(nb):
+            pltpu.make_async_copy(w_in.at[0, k, :, pl.ds(j * hid, hid)], wi_s.at[k, j], wsem.at[k, 1]).start()
+
+    def w_in_wait(k):
+        pltpu.make_async_copy(wi_s.at[k], wi_s.at[k], wsem.at[k, 1]).wait()
+
+    def h_start(part):
+        def one(i, carry):
+            k = 1 - i // nq
+            q = i % nq
+            pltpu.make_async_copy(h_saved.at[0, pl.ds(2 * part, 2), k, :, pl.ds(pl.multiple_of(q * cw, 128), cw)],
+                                  rm_s.at[k, COLS + q, pl.ds(2 * part, 2)], hsem.at[part]).start()
+            return carry
+        lax.fori_loop(0, 2 * nq, one, 0)
+
+    def h_wait(part):
+        where = rm_s.at[:, pl.ds(COLS, nq), pl.ds(2 * part, 2)]
+        pltpu.make_async_copy(where, where, hsem.at[part]).wait()
+
+    def dy_start():
+        for n in range(TILES):
+            pltpu.make_async_copy(dy_in.at[0, :, pl.ds(n * tile, tile)], cb_s.at[0, n], dysem).start()
+
+    def dy_wait():
+        pltpu.make_async_copy(cb_s.at[0], cb_s.at[0], dysem).wait()
+
+    x_copy = pltpu.make_async_copy(x_saved.at[0], xs_s, xsem)
 
     def acc_where(c):
         k = 1 - c // per_layer
@@ -91,23 +113,14 @@
     def acc_wait(c):
         acc_copies(c)[2].wait()
 
-    dy_copy.start()
+    dy_start()
+    h_start(0)
     for k in (1, 0):
-        for q in range(nq):
-            h_copy(k, 0, q).start()
-        for which in (0, 1):
-            for cp in w_copy(k, which):
-                cp.start()
-    x_copy().start()
-
-    def h_rest(i, carry):
-        k = 1 - i % 2
-        t = 1 + i // 2
-        for q in range(nq):
-            h_copy(k, t, q).start()
-        return carry
-
-    lax.fori_loop(0, 2 * (stages - 1), h_rest, 0)
+        w_out_copy(k).start()
+        w_in_start(k)
+    x_copy.start()
+    for part in range(1, stages // 2):
+        h_start(part)
     acc_start(0)
 
     barrier = pltpu.get_barrier_semaphore()
@@ -115,120 +128,114 @@
         pl.semaphore_signal(barrier, inc=1, **dev(pp, other))
     for step in range(1, stages):
         pl.semaphore_signal(barrier, inc=1, **dev((pp + step) % stages, dp))
-    pl.semaphore_wait(barrier, 3 + stages - 1)
-
-    def cot_copy(t):
-        return pltpu.make_async_remote_copy(src_ref=cb_s.at[t], dst_ref=cb_s.at[t + 1], send_sem=cot_send.at[t], recv_sem=cot_recv.at[t + 1],
+
+    def cot_copy(t, n):
+        return pltpu.make_async_remote_copy(src_ref=cb_s.at[t, n], dst_ref=cb_s.at[t + 1, n], send_sem=cot_send.at[t, n], recv_sem=cot_recv.at[t + 1, n],
                                             **dev(jnp.maximum(pp - 1, 0), dp))
 
-    def cot_arrival(t):
-        return pltpu.make_async_remote_copy(src_ref=cb_s.at[t], dst_ref=cb_s.at[t], send_sem=cot_send.at[0], recv_sem=cot_recv.at[t],
+    def cot_arrival(t, n):
+        return pltpu.make_async_remote_copy(src_ref=cb_s.at[t, n], dst_ref=cb_s.at[t, n], send_sem=cot_send.at[0, n], recv_sem=cot_recv.at[t, n],
                                             **dev(jnp.maximum(pp - 1, 0), dp))
 
-    def dx_copy(t):
-        return pltpu.make_async_remote_copy(src_ref=cb_s.at[t], dst_ref=dx_ref.at[0], send_sem=dx_send.at[t], recv_sem=dx_recv,
+    def dx_copy(t, n):
+        return pltpu.make_async_remote_copy(src_ref=cb_s.at[t, n], dst_ref=dx_ref.at[0, :, pl.ds(n * tile, tile)], send_sem=dx_send.at[t, n], recv_sem=dx_recv.at[n],
                                             **dev(t, dp))
 
-    def layer(t, k, cot):
-        rows = pl.ds(pl.multiple_of(t * tok, tok), tok)
+    def cot_now(t):
+        return jnp.concatenate([cb_s[t, n] for n in range(TILES)], axis=1)
+
+    def keep_cot(t, k, cot):
         for j in range(COLS):
-            rm_s[k, j, rows, :] = cot[:, j * cw:(j + 1) * cw]
-        back = cot.astype(F32)
-        for q in range(nq):
-            e = lax.dot_general(cot, wo_s[k, q * cw:(q + 1) * cw, :], NT, preferred_element_type=F32)
-            _, slope = gelu_and_slope(rm_s[k, COLS + q, rows, :].astype(F32))
-            dh = (e * slope).astype(BF16)
-            rm_s[k, COLS + q, rows, :] = dh
-            back += lax.dot_general(dh, wi_s[k, q], NT, preferred_element_type=F32)
-        return back.astype(BF16)
-
-    def prepare(half):
-        cols = pl.ds(half * 2 * tok, 2 * tok)
-
-        def one_layer(k, carry):
-            xx = jnp.concatenate([xs_s[2 * half, k], xs_s[2 * half + 1, k]], axis=0)
-            lt_s[k, 0, :, cols] = xx.T
-            return carry
-
-        lax.fori_loop(0, 2, one_layer, 0)
-
-    def chain_step(t, carry):
-        active = pp + t < stages
-
-        first = isinstance(t, int)
-        if first:
-            dy_copy.wait()
-        else:
-            @pl.when(active)
-            def _():
-                cot_arrival(t).wait_recv()
-
-        @pl.when(active)
-        def _():
-            def one(i, cot_idx):
-                k = 1 - i
-
-                if first:
-                    for which in (0, 1):
-                        for cp in w_copy(k, which):
-                            cp.wait()
-                cot = cb_s[t]
-                out = layer(t, k, cot)
-                cb_s[t] = out
-                return cot_idx
-            lax.fori_loop(0, 2, one, 0)
-
-            @pl.when(pp > 0)
-            def _():
-                cot_copy(t).start()
-
-            if not first:
-                @pl.when(pp == 0)
+            rm_s[k, j, t] = cot[:, j * cw:(j + 1) * cw]
+
+    def layer(t, k, sends):
+        cot = cot_now(t)
+        keep_cot(t, k, cot)
+        for j in range(nb):
+            e = lax.dot_general(cot, wo_s[k, j * hid:(j + 1) * hid, :], NT, preferred_element_type=F32)
+            for i in range(COLS):
+                q = j * COLS + i
+                _, slope = gelu_and_slope(rm_s[k, COLS + q, t].astype(F32))
+                rm_s[k, COLS + q, t] = (e[:, i * cw:(i + 1) * cw] * slope).astype(BF16)
+        for n in range(TILES):
+            back = cot[:, n * tile:(n + 1) * tile].astype(F32)
+            for j in range(nb):
+                dh = jnp.concatenate([rm_s[k, COLS + j * COLS + i, t] for i in range(COLS)], axis=1)
+                back += lax.dot_general(dh, wi_s[k, j, n * tile:(n + 1) * tile, :], NT, preferred_element_type=F32)
+            cb_s[t, n] = back.astype(BF16)
+            if sends:
+                @pl.when(pp > 0)
                 def _():
-                    dx_copy(t).start()
-
-        return carry
-
-    def h_wait(i, carry):
-        for q in range(nq):
-            h_copy(1 - i % 2, i // 2, q).wait()
-        return carry
-
-    def zero_inactive(t, carry):
-        @pl.when(pp + t >= stages)
-        def _():
-            rows = pl.ds(pl.multiple_of(t * tok, tok), tok)
-            zero = jnp.zeros((tok, cw), BF16)
-
-            def one_layer(k, c2):
-                for j in range(COLS + nq):
-                    rm_s[k, j, rows, :] = zero
-                return c2
-            lax.fori_loop(0, 2, one_layer, 0)
-        return carry
-
-    def acts(half):
+                    cot_copy(t, n).start()
+
+                if not isinstance(t, int):
+                    @pl.when(pp == 0)
+                    def _():
+                        dx_copy(t, n).start()
+
+    def layers(t):
+        layer(t, 1, False)
+        layer(t, 0, True)
+
+    def cot_wait(t):
+        for n in range(TILES):
+            cot_arrival(t, n).wait_recv()
+
+    def prepare(k, carry):
+        lt_s[k, 0] = jnp.concatenate([xs_s[t, k] for t in range(stages)], axis=0).T
+        return carry
+
+    def acts(part):
         def body(i, carry):
             k = 1 - i // nq
             q = i % nq
-            cols = pl.ds(half * 2 * tok, 2 * tok)
-            hh = rm_s[k, COLS + q, pl.ds(half * 2 * tok, 2 * tok), :].astype(F32)
+            hh = rm_s[k, COLS + q, 2 * part:2 * part + 2].reshape(2 * tok, cw).astype(F32)
             act, _ = gelu_and_slope(hh)
-            lt_s[k, 1 + q // COLS, pl.ds(pl.multiple_of((q % COLS) * cw, 128), cw), cols] = act.astype(BF16).T
+            lt_s[k, 1 + q // COLS, pl.ds(pl.multiple_of((q % COLS) * cw, 128), cw), 2 * part * tok:2 * (part + 1) * tok] = act.astype(BF16).T
             return carry
         lax.fori_loop(0, 2 * nq, body, 0)
 
-    lax.fori_loop(0, 4, h_wait, 0)
+    def zero_inactive(t, carry):
+        zero = jnp.zeros((tok, cw), BF16)
+
+        def one_layer(k, c2):
+            for j in range(COLS + nq):
+                rm_s[k, j, t] = zero
+            return c2
+        return lax.fori_loop(0, 2, one_layer, carry)
+
+    last = stages - 1 - pp
+    h_wait(0)
     acts(0)
-    chain_step(0, 0)
-    lax.fori_loop(4, 2 * stages, h_wait, 0)
-    x_copy().wait()
-    for half in range(1, stages // 2):
-        acts(half)
-    for half in range(stages // 2):
-        prepare(half)
-    lax.fori_loop(1, stages, zero_inactive, 0)
-    lax.fori_loop(1, stages, chain_step, 0)
+    dy_wait()
+    pl.semaphore_wait(barrier, 3 + stages - 1)
+    w_out_copy(1).wait()
+    w_in_wait(1)
+    layer(0, 1, False)
+    w_out_copy(0).wait()
+    w_in_wait(0)
+    layer(0, 0, True)
+    x_copy.wait()
+    lax.fori_loop(0, 2, prepare, 0)
+    for part in range(1, stages // 2):
+        h_wait(part)
+
+    def middle(t, carry):
+        cot_wait(t)
+        layers(t)
+        for part in range(1, stages // 2):
+            @pl.when(t == 2 * part - 1)
+            def _():
+                acts(part)
+        return carry
+
+    lax.fori_loop(1, jnp.where(pp == 0, stages - 1, last + 1), middle, 0)
+
+    @pl.when(last == 0)
+    def _():
+        for part in range(1, stages // 2):
+            acts(part)
+    lax.fori_loop(last + 1, stages, zero_inactive, 0)
 
     half = hid // 2
     hb = core * half
@@ -239,7 +246,7 @@
         return pl.ds(pl.multiple_of(start, 16), n)
 
     def remote(kind, c, src, dst, target):
-        return pltpu.make_async_remote_copy(src_ref=src, dst_ref=dst, send_sem=send_sem.at[kind, c % RING], recv_sem=recv_sem.at[kind, c], **dev(pp, target))
+        return pltpu.make_async_remote_copy(src_ref=src, dst_ref=dst, send_sem=send_sem.at[kind, c % RING], recv_sem=recv_sem.at[kind, c % RECV_RING], **dev(pp, target))
 
     def msg(kind, c, arriving=False):
         f = 1 if arriving else 0
@@ -296,10 +303,11 @@
         li = (1 - kind) * (1 + jj // COLS)
         ri = (1 - kind) * (jj % COLS) + kind * (COLS + jj)
         slot = c % 2
+        right = rm_s[k, ri].reshape(rows4, cw)
         nr = hid // 6 if hid % 768 == 0 else hid // 2
         for i in range(hid // nr):
             r = pl.ds(i * nr, nr)
-            g = jnp.dot(lt_s[k, li, r, :], rm_s[k, ri], preferred_element_type=F32)
+            g = jnp.dot(lt_s[k, li, r, :], right, preferred_element_type=F32)
             m_ref[c, r, :] = (acc_s[slot, r, :] + g).astype(BF16)
         send(0, c)
 
@@ -342,7 +350,7 @@
     def stage6(c):
         arrive(9, c)
 
-    plan = ((stage6, 9), (stage5, 8), (stage4, 6), (stage3, 5), (stage2, 3), (stage1, 1), (produce, 0))
+    plan = ((stage6, 16), (stage5, 14), (stage4, 11), (stage3, 8), (stage2, 5), (stage1, 2), (produce, 0))
     depth = max(lag for _, lag in plan)
 
     def run(i, carry):
@@ -354,7 +362,20 @@
                 fn(c)
         return carry
 
-    lax.fori_loop(0, total + depth, run, 0)
+    def finish(i, carry):
+        @pl.when(i == EARLY)
+        def _():
+            @pl.when(pp == 0)
+            def _():
+                layers(jnp.int32(stages - 1))
+        run(i, carry)
+        return carry
+
+    @pl.when(pp == 0)
+    def _():
+        cot_wait(stages - 1)
+        keep_cot(stages - 1, 1, cot_now(stages - 1))
+    lax.fori_loop(0, total + depth, finish, 0)
 
     def drain(i, carry):
         for kind in range(1, 10):
@@ -365,23 +386,25 @@
 
     @pl.when(pp == 0)
     def _():
-        own = pltpu.make_async_copy(cb_s.at[0], dx_ref.at[0], dx_loc)
-        own.start()
-        own.wait()
+        for n in range(TILES):
+            pltpu.make_async_copy(cb_s.at[0, n], dx_ref.at[0, :, pl.ds(n * tile, tile)], dx_loc).start()
+        pltpu.make_async_copy(cb_s.at[0], cb_s.at[0], dx_loc).wait()
 
         def sent(t, carry):
-            dx_copy(t).wait_send()
+            for n in range(TILES):
+                dx_copy(t, n).wait_send()
             return carry
         lax.fori_loop(1, stages, sent, 0)
 
     @pl.when(pp > 0)
     def _():
-        dx_copy(0).wait_recv()
-
         def sent(t, carry):
-            cot_copy(t).wait_send()
+            for n in range(TILES):
+                cot_copy(t, n).wait_send()
             return carry
         lax.fori_loop(0, stages - pp, sent, 0)
+        for n in range(TILES):
+            dx_copy(0, n).wait_recv()
 
 
 def write_kernel(sizes, m_ref, gi_ref, go_ref, out_s, out_sem):
@@ -448,31 +471,31 @@
             in_specs=[any_spec] * 7,
             out_specs=(vm_spec, vm_spec),
             scratch_shapes=[
-                pltpu.VMEM((2, nq, hid, cw), BF16),
+                pltpu.VMEM((2, ff // hid, hid, hid), BF16),
                 pltpu.VMEM((2, ff, hid), BF16),
                 pltpu.VMEM((2, 1 + ff // hid, hid, stages * tok), BF16),
-                pltpu.VMEM((2, COLS + nq, stages * tok, cw), BF16),
+                pltpu.VMEM((2, COLS + nq, stages, tok, cw), BF16),
                 pltpu.VMEM((stages, 2, tok, hid), BF16),
-                pltpu.VMEM((stages, tok, hid), BF16),
+                pltpu.VMEM((stages, TILES, tok, hid // TILES), BF16),
                 pltpu.VMEM((2, hid, cw), F32),
                 pltpu.VMEM((total, hid // 2, cw), BF16),
                 pltpu.VMEM((total, 2, 2 * unit, cw), BF16),
                 pltpu.VMEM((total, 2, unit, cw), BF16),
-                pltpu.SemaphoreType.DMA((2, 1 + nq)),
-                pltpu.SemaphoreType.DMA((2, stages, nq)),
+                pltpu.SemaphoreType.DMA((2, 2)),
+                pltpu.SemaphoreType.DMA((stages // 2,)),
                 pltpu.SemaphoreType.DMA,
                 pltpu.SemaphoreType.DMA,
                 pltpu.SemaphoreType.DMA((2,)),
-                pltpu.SemaphoreType.DMA((stages,)),
-                pltpu.SemaphoreType.DMA((stages,)),
-                pltpu.SemaphoreType.DMA((stages,)),
-                pltpu.SemaphoreType.DMA,
+                pltpu.SemaphoreType.DMA((stages, TILES)),
+                pltpu.SemaphoreType.DMA((stages, TILES)),
+                pltpu.SemaphoreType.DMA((stages, TILES)),
+                pltpu.SemaphoreType.DMA((TILES,)),
                 pltpu.SemaphoreType.DMA,
                 pltpu.SemaphoreType.DMA((10, RING)),
-                pltpu.SemaphoreType.DMA((10, total)),
+                pltpu.SemaphoreType.DMA((10, RECV_RING)),
                 pltpu.SemaphoreType.REGULAR,
             ],
-            compiler_params=pltpu.CompilerParams(collective_id=0, has_side_effects=True, vmem_limit_bytes=46720 * 1024),
+            compiler_params=pltpu.CompilerParams(collective_id=0, has_side_effects=True, vmem_limit_bytes=46900 * 1024),
             name='chain_reduce',
         )(w_in, w_out, x_saved, h_saved, dy_in, acc_in, acc_out)
         grad_in, grad_out = pl.pallas_call(

time: 233 us -> 214 us (0.918)
  Pallas kernels: 231 us -> 212 us
    pallas_call x1, Pallas kernels: 219 us -> 200 us  [device_fn(): pl.pallas_call(functools.partial(main_kernel, sizes), out_shape=(pltpu.VM...]
where the time goes in v2:
time: 214 us; the launch traced here: 213 us
  Pallas kernels  212 us (99%)
    pallas_call x1, Pallas kernels, device_fn(): pl.pallas_call(functools.partial(main_kernel, sizes), out_shape=(pltpu.VM...  200 us
    pallas_call x1, Pallas kernels, device_fn(): pl.pallas_call(functools.partial(write_kernel, sizes), out_shape=(jax.Sha...  12.3 us

profile of v2, /device:TPU:0, one launch (start us, length us, event | category | flops | bytes accessed | tf_op | source)
XLA Modules:
  0.0 213.3 jit_solution(7112003614197301561)
XLA Ops:
  0.6 199.8 %chain_reduce.1 = (bf16[32,768,384]{2,1,0:T(8,128)(2,1)S(1)}, bf16[1,64,768]{2,1,0:T(8,128)(2,1)}) custom-call(bf16[1,2,768,3072]{3,2,1,0:T(8,128)(2,1)} %w_in.1, bf16[1,2,3072,768]{3,2,1,0:T(8,128)(2,1)} %w_out.1, bf16[1,4,2,64,768]{4,3,2,1,0:T(8,128)(2,1)} %x_saved.1, bf16[1,4,2,64,3072]{4,3,2,1,0:T(8,128)(2,1)} %h_saved.1, bf16[1,64,768]{2,1,0:T(8,128)(2,1)} %dy_in.1, ...), custom_call_target="tpu_custom_call" | custom-call | tf_op jit(solution)/shard_map/chain_reduce/pallas_call | solution.py:468
  200.4 0.0 copy-start
  200.4 12.3 %write_out.1 = (f32[1,2,768,3072]{3,2,1,0:T(8,128)}, f32[1,2,3072,768]{3,2,1,0:T(8,128)}) custom-call(bf16[32,768,384]{2,1,0:T(8,128)(2,1)S(1)} %get-tuple-element.7.m_ref), custom_call_target="tpu_custom_call" | custom-call | tf_op jit(solution)/shard_map/write_out/pallas_call | solution.py:501
  212.7 0.0 copy-done
  212.7 0.6 copy.11
Async XLA Ops:
  200.4 12.3 %copy-start = (bf16[1,64,768]{2,1,0:T(8,128)(2,1)S(1)}, bf16[1,64,768]{2,1,0:T(8,128)(2,1)}, u32[]{:S(2)}) copy-start(bf16[1,64,768]{2,1,0:T(8,128)(2,1)} %get-tuple-element.16) | copy-start | bytes 294916

commit v3 on v2

--- a/solution.py
+++ b/solution.py
@@ -13,6 +13,9 @@
 TILES = 3
 RING = 4
 RECV_RING = 8
+MOVED = (2, 1)
+POS = 20
+HAND = 9
 EARLY = 7
 
 
@@ -29,8 +32,8 @@
 def main_kernel(sizes, w_in, w_out, x_saved, h_saved, dy_in, acc_in, acc_out,
                 m_ref, dx_ref,
                 wi_s, wo_s, lt_s, rm_s, xs_s, cb_s, acc_s, p_s, h1_s, h2_s,
-                wsem, hsem, xsem, dysem, accsem, cot_send, cot_recv, dx_send, dx_recv, dx_loc,
-                send_sem, recv_sem, free_sem):
+                wsem, hsem, xsem, dysem, accsem, cot_send, cot_recv,
+                send_sem, recv_sem, free_sem, mv_send, mv_recv, z_free, mv_free):
     hid, ff, tok, stages = sizes
     cw = hid // COLS
     nq = ff // cw
@@ -91,16 +94,15 @@
         b = c % per_layer
         return k, b // per_kind, b % per_kind
 
-    def acc_copies(c):
+    def acc_copies(c, slot):
         k, kind, jj = acc_where(c)
-        slot = c % 2
         a = pltpu.make_async_copy(acc_out.at[0, 0, k, pl.ds(pl.multiple_of((jj // COLS) * hid, 128), hid), pl.ds(pl.multiple_of((jj % COLS) * cw, 128), cw)],
                                   acc_s.at[slot], accsem.at[slot])
         b = pltpu.make_async_copy(acc_in.at[0, 0, k, :, pl.ds(pl.multiple_of(jj * cw, 128), cw)], acc_s.at[slot], accsem.at[slot])
         return kind, a, b
 
-    def acc_start(c):
-        kind, a, b = acc_copies(c)
+    def acc_start(c, slot):
+        kind, a, b = acc_copies(c, slot)
 
         @pl.when(kind == 0)
         def _():
@@ -110,8 +112,8 @@
         def _():
             b.start()
 
-    def acc_wait(c):
-        acc_copies(c)[2].wait()
+    def acc_wait(slot):
+        pltpu.make_async_copy(acc_s.at[slot], acc_s.at[slot], accsem.at[slot]).wait()
 
     dy_start()
     h_start(0)
@@ -121,7 +123,7 @@
     x_copy.start()
     for part in range(1, stages // 2):
         h_start(part)
-    acc_start(0)
+    acc_start(0, 0)
 
     barrier = pltpu.get_barrier_semaphore()
     for other in (pair, xn, yn):
@@ -130,16 +132,15 @@
         pl.semaphore_signal(barrier, inc=1, **dev((pp + step) % stages, dp))
 
     def cot_copy(t, n):
-        return pltpu.make_async_remote_copy(src_ref=cb_s.at[t, n], dst_ref=cb_s.at[t + 1, n], send_sem=cot_send.at[t, n], recv_sem=cot_recv.at[t + 1, n],
-                                            **dev(jnp.maximum(pp - 1, 0), dp))
+        above = pp > 0
+        spare = (stages - 1, stages - 2) if isinstance(t, int) else (t, stages - 1)
+        slot = jnp.where(above, t + 1, spare[1])
+        return pltpu.make_async_remote_copy(src_ref=cb_s.at[t, n], dst_ref=cb_s.at[slot, n], send_sem=cot_send.at[t, n], recv_sem=cot_recv.at[slot, n],
+                                            **dev(jnp.where(above, pp - 1, spare[0]), dp))
 
     def cot_arrival(t, n):
         return pltpu.make_async_remote_copy(src_ref=cb_s.at[t, n], dst_ref=cb_s.at[t, n], send_sem=cot_send.at[0, n], recv_sem=cot_recv.at[t, n],
                                             **dev(jnp.maximum(pp - 1, 0), dp))
-
-    def dx_copy(t, n):
-        return pltpu.make_async_remote_copy(src_ref=cb_s.at[t, n], dst_ref=dx_ref.at[0, :, pl.ds(n * tile, tile)], send_sem=dx_send.at[t, n], recv_sem=dx_recv.at[n],
-                                            **dev(t, dp))
 
     def cot_now(t):
         return jnp.concatenate([cb_s[t, n] for n in range(TILES)], axis=1)
@@ -164,14 +165,7 @@
                 back += lax.dot_general(dh, wi_s[k, j, n * tile:(n + 1) * tile, :], NT, preferred_element_type=F32)
             cb_s[t, n] = back.astype(BF16)
             if sends:
-                @pl.when(pp > 0)
-                def _():
-                    cot_copy(t, n).start()
-
-                if not isinstance(t, int):
-                    @pl.when(pp == 0)
-                    def _():
-                        dx_copy(t, n).start()
+                cot_copy(t, n).start()
 
     def layers(t):
         layer(t, 1, False)
@@ -241,170 +235,283 @@
     hb = core * half
     xb = hb
     yb = hb + 4 * unit
+    zp = stages - 1 - pp
+    helper = pp >= stages // 2
+    moved = jnp.where((pp == 0) | (pp == stages - 1), MOVED[0], MOVED[1])
+    steps = jnp.where(helper, total + moved, total - moved)
+    own = jnp.where(helper, total, total - moved)
+
+    def is_foreign(i):
+        return helper & (i >= POS) & (i < POS + moved)
+
+    def own_of(i):
+        return jnp.where(helper & (i >= POS), i - moved, i)
 
     def rows_of(start, n):
         return pl.ds(pl.multiple_of(start, 16), n)
 
-    def remote(kind, c, src, dst, target):
-        return pltpu.make_async_remote_copy(src_ref=src, dst_ref=dst, send_sem=send_sem.at[kind, c % RING], recv_sem=recv_sem.at[kind, c % RECV_RING], **dev(pp, target))
-
-    def msg(kind, c, arriving=False):
+    def msg(kind, i, foreign, arriving=False):
         f = 1 if arriving else 0
+        c = i - POS if foreign else own_of(i)
+
+        def remote(src, dst, target):
+            j = c if kind in (0, 9) else i
+            return pltpu.make_async_remote_copy(src_ref=src, dst_ref=dst, send_sem=send_sem.at[kind, j % RING], recv_sem=recv_sem.at[kind, j % RECV_RING], **dev(pp, target))
+
+        def place(start, n):
+            return p_s.at[c, rows_of(start, n), :] if foreign else m_ref.at[c, rows_of(hb + start, n), :]
+        yp = 4 * unit
         if kind == 0:
-            other = m_ref.at[c, rows_of(half - hb, half), :]
-            return remote(0, c, other, p_s.at[c], pair)
+            return remote(m_ref.at[c, rows_of(half - hb, half), :], p_s.at[c], pair)
         if kind == 1:
-            return remote(1, c, p_s.at[c, rows_of((1 - xc) * 2 * unit, 2 * unit), :], h1_s.at[c, 0], xn)
+            return remote(p_s.at[c, rows_of((1 - xc) * 2 * unit, 2 * unit), :], h1_s.at[c, 0], xn)
         if kind == 2:
-            return remote(2, c, p_s.at[c, rows_of(4 * unit + (1 - yc) * 2 * unit, 2 * unit), :], h1_s.at[c, 1], yn)
+            return remote(p_s.at[c, rows_of(yp + (1 - yc) * 2 * unit, 2 * unit), :], h1_s.at[c, 1], yn)
         if kind == 3:
-            return remote(3, c, h1_s.at[c, 0, rows_of((1 - yc) * unit, unit), :], h2_s.at[c, 0], yn)
+            return remote(h1_s.at[c, 0, rows_of((1 - yc) * unit, unit), :], h2_s.at[c, 0], yn)
         if kind == 4:
-            return remote(4, c, h1_s.at[c, 1, rows_of((1 - xc) * unit, unit), :], h2_s.at[c, 1], xn)
+            return remote(h1_s.at[c, 1, rows_of((1 - xc) * unit, unit), :], h2_s.at[c, 1], xn)
         if kind == 5:
             y_of = 1 - yc if f else yc
-            r = m_ref.at[c, rows_of(xb + xc * 2 * unit + y_of * unit, unit), :]
-            return remote(5, c, r, r, yn)
+            r = place(xc * 2 * unit + y_of * unit, unit)
+            return remote(r, r, yn)
         if kind == 6:
             x_of = 1 - xc if f else xc
-            r = m_ref.at[c, rows_of(yb + yc * 2 * unit + x_of * unit, unit), :]
-            return remote(6, c, r, r, xn)
+            r = place(yp + yc * 2 * unit + x_of * unit, unit)
+            return remote(r, r, xn)
         if kind == 7:
             x_of = 1 - xc if f else xc
-            r = m_ref.at[c, rows_of(xb + x_of * 2 * unit, 2 * unit), :]
-            return remote(7, c, r, r, xn)
+            r = place(x_of * 2 * unit, 2 * unit)
+            return remote(r, r, xn)
         if kind == 8:
             y_of = 1 - yc if f else yc
-            r = m_ref.at[c, rows_of(yb + y_of * 2 * unit, 2 * unit), :]
-            return remote(8, c, r, r, yn)
-        base = half - hb if f else hb
-        r = m_ref.at[c, rows_of(base, half), :]
-        return remote(9, c, r, r, pair)
-
-    def send(kind, c):
-        if kind > 0:
-            @pl.when(c >= RING)
+            r = place(yp + y_of * 2 * unit, 2 * unit)
+            return remote(r, r, yn)
+        r = m_ref.at[c, rows_of(half - hb if f else hb, half), :]
+        return remote(r, r, pair)
+
+    def moved_msg(kind, f, arriving=False):
+        c = total - moved + f
+
+        def remote(src, dst, pp_i, dp_i):
+            return pltpu.make_async_remote_copy(src_ref=src, dst_ref=dst, send_sem=mv_send.at[kind, f], recv_sem=mv_recv.at[kind, f], **dev(pp_i, dp_i))
+        if kind == 0:
+            return remote(m_ref.at[c, rows_of(half - hb, half), :], p_s.at[c], pp, pair)
+        if kind == 1:
+            return remote(p_s.at[c], p_s.at[f], zp, dp)
+        if kind == 2:
+            return remote(p_s.at[f], m_ref.at[c, rows_of(hb, half), :], zp, dp)
+        r = m_ref.at[c, rows_of(half - hb if arriving else hb, half), :]
+        return remote(r, r, pp, pair)
+
+    def send(kind, i, foreign):
+        if kind >= 3:
+            j = own_of(i) if kind == 9 else i
+
+            @pl.when(j >= RING)
             def _():
-                msg(kind, c - RING).wait_send()
-        msg(kind, c).start()
-
-    def arrive(kind, c):
-        msg(kind, c, True).wait_recv()
+                wait_sent(kind, i)
+        msg(kind, i, foreign).start()
+
+    def wait_sent(kind, i):
+        msg(kind, i, False).wait_send()
+
+    def arrive(kind, i, foreign):
+        msg(kind, i, foreign, True).wait_recv()
 
     def plus(left, right):
         return (left.astype(F32) + right.astype(F32)).astype(BF16)
 
-    def produce(c):
-        @pl.when(c + 1 < total)
-        def _():
-            acc_start(c + 1)
-        acc_wait(c)
+    def product(c, slot):
         k, kind, jj = acc_where(c)
         li = (1 - kind) * (1 + jj // COLS)
         ri = (1 - kind) * (jj % COLS) + kind * (COLS + jj)
-        slot = c % 2
         right = rm_s[k, ri].reshape(rows4, cw)
         nr = hid // 6 if hid % 768 == 0 else hid // 2
-        for i in range(hid // nr):
-            r = pl.ds(i * nr, nr)
+        for n in range(hid // nr):
+            r = pl.ds(n * nr, nr)
             g = jnp.dot(lt_s[k, li, r, :], right, preferred_element_type=F32)
             m_ref[c, r, :] = (acc_s[slot, r, :] + g).astype(BF16)
-        send(0, c)
-
-    def stage1(c):
-        arrive(0, c)
+
+    def produce(i, foreign):
+        if foreign:
+            return
+        c = own_of(i)
+
+        @pl.when(c + 1 < own)
+        def _():
+            acc_start(c + 1, (c + 1) % 2)
+        acc_wait(c % 2)
+        product(c, c % 2)
+        send(0, i, False)
+
+    def stage1(i, foreign):
+        if foreign:
+            f = i - POS
+            moved_msg(1, f, True).wait_recv()
+            send(1, i, True)
+            send(2, i, True)
+            return
+        c = own_of(i)
+        arrive(0, i, False)
         p_s[c] = plus(p_s[c], m_ref[c, rows_of(hb, half), :])
-        send(1, c)
-        send(2, c)
-        msg(0, c).wait_send()
+        send(1, i, False)
+        send(2, i, False)
+        wait_sent(0, i)
         pl.semaphore_signal(free_sem, inc=1, **dev(pp, pair))
 
-    def stage2(c):
-        arrive(1, c)
+    def stage2(i, foreign):
+        c = i - POS if foreign else own_of(i)
+        arrive(1, i, foreign)
         h1_s[c, 0] = plus(h1_s[c, 0], p_s[c, rows_of(xc * 2 * unit, 2 * unit), :])
-        send(3, c)
-        arrive(2, c)
+        wait_sent(2, i)
+        send(3, i, foreign)
+        arrive(2, i, foreign)
         h1_s[c, 1] = plus(h1_s[c, 1], p_s[c, rows_of(4 * unit + yc * 2 * unit, 2 * unit), :])
-        send(4, c)
-
-    def stage3(c):
-        arrive(3, c)
-        m_ref[c, rows_of(xb + xc * 2 * unit + yc * unit, unit), :] = plus(h1_s[c, 0, rows_of(yc * unit, unit), :], h2_s[c, 0])
-        send(5, c)
-        arrive(4, c)
-        m_ref[c, rows_of(yb + yc * 2 * unit + xc * unit, unit), :] = plus(h1_s[c, 1, rows_of(xc * unit, unit), :], h2_s[c, 1])
-        send(6, c)
-
-    def stage4(c):
-        arrive(5, c)
-        send(7, c)
-        arrive(6, c)
-        send(8, c)
-
-    def stage5(c):
-        arrive(7, c)
-        arrive(8, c)
+        wait_sent(1, i)
+        send(4, i, foreign)
+        if not foreign:
+            @pl.when(helper & (i < moved))
+            def _():
+                pl.semaphore_signal(z_free, inc=1, **dev(zp, dp))
+
+    def stage3(i, foreign):
+        c = i - POS if foreign else own_of(i)
+
+        def keep(start, value):
+            if foreign:
+                p_s[c, rows_of(start, unit), :] = value
+            else:
+                m_ref[c, rows_of(hb + start, unit), :] = value
+        arrive(3, i, foreign)
+        keep(xc * 2 * unit + yc * unit, plus(h1_s[c, 0, rows_of(yc * unit, unit), :], h2_s[c, 0]))
+        send(5, i, foreign)
+        arrive(4, i, foreign)
+        keep(4 * unit + yc * 2 * unit + xc * unit, plus(h1_s[c, 1, rows_of(xc * unit, unit), :], h2_s[c, 1]))
+        send(6, i, foreign)
+
+    def stage4(i, foreign):
+        arrive(5, i, foreign)
+        send(7, i, foreign)
+        arrive(6, i, foreign)
+        send(8, i, foreign)
+
+    def stage5(i, foreign):
+        arrive(7, i, foreign)
+        arrive(8, i, foreign)
+        if foreign:
+            moved_msg(2, i - POS).start()
+            return
         pl.semaphore_wait(free_sem, 1)
-        send(9, c)
-
-    def stage6(c):
-        arrive(9, c)
+        send(9, i, False)
+
+    def stage6(i, foreign):
+        if not foreign:
+            arrive(9, i, False)
 
     plan = ((stage6, 16), (stage5, 14), (stage4, 11), (stage3, 8), (stage2, 5), (stage1, 2), (produce, 0))
     depth = max(lag for _, lag in plan)
 
-    def run(i, carry):
+    def run(i):
         for fn, lag in plan:
-            c = i - lag
-
-            @pl.when((c >= 0) & (c < total))
+            j = i - lag
+            live = (j >= 0) & (j < steps)
+
+            @pl.when(live & jnp.logical_not(is_foreign(j)))
             def _():
-                fn(c)
-        return carry
-
-    def finish(i, carry):
-        @pl.when(i == EARLY)
-        def _():
-            @pl.when(pp == 0)
+                fn(j, False)
+
+            if fn not in (produce, stage6):
+                @pl.when(live & is_foreign(j))
+                def _():
+                    fn(j, True)
+
+    def hand_over(i):
+        @pl.when((i >= HAND) & (i < HAND + moved))
+        def _():
+            f = i - HAND
+            c = total - moved + f
+            acc_start(c, i % 2)
+            acc_wait(i % 2)
+            product(c, i % 2)
+            moved_msg(0, f).start()
+
+        @pl.when((i >= HAND + 2) & (i < HAND + 2 + moved))
+        def _():
+            f = i - HAND - 2
+            c = total - moved + f
+            moved_msg(0, f).wait_recv()
+            p_s[c] = plus(p_s[c], m_ref[c, rows_of(hb, half), :])
+            moved_msg(0, f).wait_send()
+            pl.semaphore_signal(mv_free, inc=1, **dev(pp, pair))
+            pl.semaphore_wait(z_free, 1)
+            moved_msg(1, f).start()
+
+    def step(i, carry):
+        @pl.when(pp == 0)
+        def _():
+            @pl.when(i == EARLY)
             def _():
                 layers(jnp.int32(stages - 1))
-        run(i, carry)
+        run(i)
+
+        @pl.when(jnp.logical_not(helper))
+        def _():
+            hand_over(i)
         return carry
 
     @pl.when(pp == 0)
     def _():
         cot_wait(stages - 1)
         keep_cot(stages - 1, 1, cot_now(stages - 1))
-    lax.fori_loop(0, total + depth, finish, 0)
+    lax.fori_loop(0, steps + depth, step, 0)
+
+    @pl.when(jnp.logical_not(helper))
+    def _():
+        def give(f, carry):
+            moved_msg(2, f).wait_recv()
+            pl.semaphore_wait(mv_free, 1)
+            moved_msg(3, f).start()
+            return carry
+        lax.fori_loop(0, moved, give, 0)
+
+        def take(f, carry):
+            moved_msg(3, f, True).wait_recv()
+            moved_msg(3, f).wait_send()
+            moved_msg(1, f).wait_send()
+            return carry
+        lax.fori_loop(0, moved, take, 0)
+
+    @pl.when(helper)
+    def _():
+        def back(f, carry):
+            moved_msg(2, f).wait_send()
+            return carry
+        lax.fori_loop(0, moved, back, 0)
 
     def drain(i, carry):
-        for kind in range(1, 10):
-            msg(kind, total - RING + i).wait_send()
+        for kind in range(3, 10):
+            msg(kind, steps - RING + i, False).wait_send()
         return carry
 
     lax.fori_loop(0, RING, drain, 0)
-
-    @pl.when(pp == 0)
-    def _():
-        for n in range(TILES):
-            pltpu.make_async_copy(cb_s.at[0, n], dx_ref.at[0, :, pl.ds(n * tile, tile)], dx_loc).start()
-        pltpu.make_async_copy(cb_s.at[0], cb_s.at[0], dx_loc).wait()
-
-        def sent(t, carry):
-            for n in range(TILES):
-                dx_copy(t, n).wait_send()
-            return carry
-        lax.fori_loop(1, stages, sent, 0)
 
     @pl.when(pp > 0)
     def _():
-        def sent(t, carry):
-            for n in range(TILES):
-                cot_copy(t, n).wait_send()
-            return carry
-        lax.fori_loop(0, stages - pp, sent, 0)
+        cot_wait(stages - 1)
+
+    @pl.when(pp == stages - 1)
+    def _():
+        cot_wait(stages - 2)
+
+    def sent(t, carry):
         for n in range(TILES):
-            dx_copy(0, n).wait_recv()
+            cot_copy(t, n).wait_send()
+        return carry
+    lax.fori_loop(0, stages - pp, sent, 0)
+    out_slot = jnp.where(pp == 0, 0, stages - 1)
+    for n in range(TILES):
+        dx_ref[0, :, n * tile:(n + 1) * tile] = cb_s[out_slot, n]
 
 
 def write_kernel(sizes, m_ref, gi_ref, go_ref, out_s, out_sem):
@@ -488,11 +595,12 @@
                 pltpu.SemaphoreType.DMA((2,)),
                 pltpu.SemaphoreType.DMA((stages, TILES)),
                 pltpu.SemaphoreType.DMA((stages, TILES)),
-                pltpu.SemaphoreType.DMA((stages, TILES)),
-                pltpu.SemaphoreType.DMA((TILES,)),
-                pltpu.SemaphoreType.DMA,
                 pltpu.SemaphoreType.DMA((10, RING)),
                 pltpu.SemaphoreType.DMA((10, RECV_RING)),
+                pltpu.SemaphoreType.REGULAR,
+                pltpu.SemaphoreType.DMA((4, max(MOVED))),
+                pltpu.SemaphoreType.DMA((4, max(MOVED))),
+                pltpu.SemaphoreType.REGULAR,
                 pltpu.SemaphoreType.REGULAR,
             ],
             compiler_params=pltpu.CompilerParams(collective_id=0, has_side_effects=True, vmem_limit_bytes=46900 * 1024),

time: 214 us -> 206 us (0.963)
  Pallas kernels: 212 us -> 205 us
    pallas_call x1, Pallas kernels: 200 us -> 192 us  [device_fn(): pl.pallas_call(functools.partial(main_kernel, sizes), out_shape=(pltpu.VM...]
where the time goes in v3:
time: 206 us
  Pallas kernels  205 us (100%)
    pallas_call x1, Pallas kernels, device_fn(): pl.pallas_call(functools.partial(main_kernel, sizes), out_shape=(pltpu.VM...  192 us
    pallas_call x1, Pallas kernels, device_fn(): pl.pallas_call(functools.partial(write_kernel, sizes), out_shape=(jax.Sha...  12.3 us

profile of v3, /device:TPU:0, one launch (start us, length us, event | category | flops | bytes accessed | tf_op | source)
XLA Modules:
  0.0 206.0 jit_solution(11543490442929171050)
XLA Ops:
  0.6 192.5 %chain_reduce.1 = (bf16[32,768,384]{2,1,0:T(8,128)(2,1)S(1)}, bf16[1,64,768]{2,1,0:T(8,128)(2,1)}) custom-call(bf16[1,2,768,3072]{3,2,1,0:T(8,128)(2,1)} %w_in.1, bf16[1,2,3072,768]{3,2,1,0:T(8,128)(2,1)} %w_out.1, bf16[1,4,2,64,768]{4,3,2,1,0:T(8,128)(2,1)} %x_saved.1, bf16[1,4,2,64,3072]{4,3,2,1,0:T(8,128)(2,1)} %h_saved.1, bf16[1,64,768]{2,1,0:T(8,128)(2,1)} %dy_in.1, ...), custom_call_target="tpu_custom_call" | custom-call | tf_op jit(solution)/shard_map/chain_reduce/pallas_call | solution.py:575
  193.1 0.0 copy-start
  193.1 12.3 %write_out.1 = (f32[1,2,768,3072]{3,2,1,0:T(8,128)}, f32[1,2,3072,768]{3,2,1,0:T(8,128)}) custom-call(bf16[32,768,384]{2,1,0:T(8,128)(2,1)S(1)} %get-tuple-element.7.m_ref), custom_call_target="tpu_custom_call" | custom-call | tf_op jit(solution)/shard_map/write_out/pallas_call | solution.py:609
  205.4 0.0 copy-done
  205.4 0.6 copy.11
Async XLA Ops:
  193.1 12.3 %copy-start = (bf16[1,64,768]{2,1,0:T(8,128)(2,1)S(1)}, bf16[1,64,768]{2,1,0:T(8,128)(2,1)}, u32[]{:S(2)}) copy-start(bf16[1,64,768]{2,1,0:T(8,128)(2,1)} %get-tuple-element.16) | copy-start | bytes 294916

commit v4 on v3

--- a/solution.py
+++ b/solution.py
@@ -9,14 +9,14 @@
 BF16 = jnp.bfloat16
 F32 = jnp.float32
 NT = (((1,), (1,)), ((), ()))
-COLS = 2
+COLS = 3
 TILES = 3
 RING = 4
 RECV_RING = 8
-MOVED = (2, 1)
-POS = 20
-HAND = 9
-EARLY = 7
+MOVED = (4, 1)
+POS = 26
+HAND = 13
+EARLY = 10
 
 
 def gelu_and_slope(h):
@@ -117,13 +117,8 @@
 
     dy_start()
     h_start(0)
-    for k in (1, 0):
-        w_out_copy(k).start()
-        w_in_start(k)
-    x_copy.start()
-    for part in range(1, stages // 2):
-        h_start(part)
-    acc_start(0, 0)
+    w_out_copy(1).start()
+    w_in_start(1)
 
     barrier = pltpu.get_barrier_semaphore()
     for other in (pair, xn, yn):
@@ -200,15 +195,21 @@
 
     last = stages - 1 - pp
     h_wait(0)
+    w_out_copy(0).start()
+    w_in_start(0)
     acts(0)
     dy_wait()
     pl.semaphore_wait(barrier, 3 + stages - 1)
     w_out_copy(1).wait()
     w_in_wait(1)
     layer(0, 1, False)
+    x_copy.start()
     w_out_copy(0).wait()
     w_in_wait(0)
     layer(0, 0, True)
+    acc_start(0, 0)
+    for part in range(1, stages // 2):
+        h_start(part)
     x_copy.wait()
     lax.fori_loop(0, 2, prepare, 0)
     for part in range(1, stages // 2):
@@ -227,8 +228,10 @@
 
     @pl.when(last == 0)
     def _():
-        for part in range(1, stages // 2):
-            acts(part)
+        def blank(i, carry):
+            lt_s[1 - i // (1 + nb), i % (1 + nb), :, 2 * tok:] = jnp.zeros((hid, (stages - 2) * tok), BF16)
+            return carry
+        lax.fori_loop(0, 2 * (1 + nb), blank, 0)
     lax.fori_loop(last + 1, stages, zero_inactive, 0)
 
     half = hid // 2
@@ -447,6 +450,15 @@
             pl.semaphore_wait(z_free, 1)
             moved_msg(1, f).start()
 
+    def give(i):
+        f = i - (steps + depth - 2 - moved)
+
+        @pl.when((f >= 0) & (f < moved))
+        def _():
+            moved_msg(2, f).wait_recv()
+            pl.semaphore_wait(mv_free, 1)
+            moved_msg(3, f).start()
+
     def step(i, carry):
         @pl.when(pp == 0)
         def _():
@@ -458,6 +470,7 @@
         @pl.when(jnp.logical_not(helper))
         def _():
             hand_over(i)
+            give(i)
         return carry
 
     @pl.when(pp == 0)
@@ -468,13 +481,6 @@
 
     @pl.when(jnp.logical_not(helper))
     def _():
-        def give(f, carry):
-            moved_msg(2, f).wait_recv()
-            pl.semaphore_wait(mv_free, 1)
-            moved_msg(3, f).start()
-            return carry
-        lax.fori_loop(0, moved, give, 0)
-
         def take(f, carry):
             moved_msg(3, f, True).wait_recv()
             moved_msg(3, f).wait_send()
@@ -514,13 +520,15 @@
         dx_ref[0, :, n * tile:(n + 1) * tile] = cb_s[out_slot, n]
 
 
-def write_kernel(sizes, m_ref, gi_ref, go_ref, out_s, out_sem):
+def write_kernel(sizes, m_ref, dx_ref, gi_ref, go_ref, dxo_ref, out_s, out_sem, dx_sem):
     hid, ff, tok, stages = sizes
     cw = hid // COLS
     nq = ff // cw
     per_layer = 2 * nq
     total = 2 * per_layer
     slots = out_s.shape[0]
+    dx_copy = pltpu.make_async_copy(dx_ref, dxo_ref, dx_sem)
+    dx_copy.start()
 
     def copies(c):
         k = 1 - c // per_layer
@@ -557,6 +565,7 @@
         copies(total - slots + i)[2].wait()
         return carry
     lax.fori_loop(0, slots, drain, 0)
+    dx_copy.wait()
 
 
 def solution(mesh):
@@ -574,7 +583,7 @@
         vm_spec = pl.BlockSpec(memory_space=pltpu.VMEM)
         m_all, dx = pl.pallas_call(
             functools.partial(main_kernel, sizes),
-            out_shape=(pltpu.VMEM((total, hid, cw), BF16), jax.ShapeDtypeStruct((1, tok, hid), BF16)),
+            out_shape=(pltpu.VMEM((total, hid, cw), BF16), pltpu.VMEM((1, tok, hid), BF16)),
             in_specs=[any_spec] * 7,
             out_specs=(vm_spec, vm_spec),
             scratch_shapes=[
@@ -606,15 +615,15 @@
             compiler_params=pltpu.CompilerParams(collective_id=0, has_side_effects=True, vmem_limit_bytes=46900 * 1024),
             name='chain_reduce',
         )(w_in, w_out, x_saved, h_saved, dy_in, acc_in, acc_out)
-        grad_in, grad_out = pl.pallas_call(
+        grad_in, grad_out, dx = pl.pallas_call(
             functools.partial(write_kernel, sizes),
-            out_shape=(jax.ShapeDtypeStruct((1, 2, hid, ff), F32), jax.ShapeDtypeStruct((1, 2, ff, hid), F32)),
-            in_specs=[vm_spec],
-            out_specs=(any_spec, any_spec),
-            scratch_shapes=[pltpu.VMEM((4, hid, cw), F32), pltpu.SemaphoreType.DMA((4,))],
+            out_shape=(jax.ShapeDtypeStruct((1, 2, hid, ff), F32), jax.ShapeDtypeStruct((1, 2, ff, hid), F32), jax.ShapeDtypeStruct((1, tok, hid), BF16)),
+            in_specs=[vm_spec, vm_spec],
+            out_specs=(any_spec, any_spec, any_spec),
+            scratch_shapes=[pltpu.VMEM((4, hid, cw), F32), pltpu.SemaphoreType.DMA((4,)), pltpu.SemaphoreType.DMA],
             compiler_params=pltpu.CompilerParams(vmem_limit_bytes=16 * 1024 * 1024),
             name='write_out',
-        )(m_all)
+        )(m_all, dx)
         return grad_in, grad_out, dx
 
     return jax.shard_map(device_fn, mesh=mesh, in_specs=(P('pp'), P('pp'), P('pp', None, None, 'dp'), P('pp', None, None, 'dp'), P('pp', 'dp'), P('pp', 'dp'), P('pp', 'dp')), out_specs=(P('pp'), P('pp'), P('pp', 'dp')), check_vma=False)

time: 206 us -> 202 us (0.981); the launches traced: 206 us -> 200 us
  Pallas kernels: 205 us -> 199 us
    pallas_call x1, Pallas kernels: 192 us -> 187 us  [device_fn(): pl.pallas_call(functools.partial(main_kernel, sizes), out_shape=(pltpu.VM...]
where the time goes in v4:
time: 202 us; the launch traced here: 200 us
  Pallas kernels  199 us (99%)
    pallas_call x1, Pallas kernels, device_fn(): pl.pallas_call(functools.partial(main_kernel, sizes), out_shape=(pltpu.VM...  187 us
    pallas_call x1, Pallas kernels, device_fn(): pl.pallas_call(functools.partial(write_kernel, sizes), out_shape=(jax.Sha...  12.2 us

profile of v4, /device:TPU:0, one launch (start us, length us, event | category | flops | bytes accessed | tf_op | source)
XLA Modules:
  0.0 199.8 jit_solution(11512508599633324140)
XLA Ops:
  0.6 186.7 %chain_reduce.1 = (bf16[48,768,256]{2,1,0:T(8,128)(2,1)S(1)}, bf16[1,64,768]{2,1,0:T(8,128)(2,1)S(1)}) custom-call(bf16[1,2,768,3072]{3,2,1,0:T(8,128)(2,1)} %w_in.1, bf16[1,2,3072,768]{3,2,1,0:T(8,128)(2,1)} %w_out.1, bf16[1,4,2,64,768]{4,3,2,1,0:T(8,128)(2,1)} %x_saved.1, bf16[1,4,2,64,3072]{4,3,2,1,0:T(8,128)(2,1)} %h_saved.1, bf16[1,64,768]{2,1,0:T(8,128)(2,1)} %dy_in.1, ...), custom_call_target="tpu_custom_call" | custom-call | tf_op jit(solution)/shard_map/chain_reduce/pallas_call | solution.py:584
  187.4 12.2 %write_out.1 = (f32[1,2,768,3072]{3,2,1,0:T(8,128)}, f32[1,2,3072,768]{3,2,1,0:T(8,128)}, bf16[1,64,768]{2,1,0:T(8,128)(2,1)}) custom-call(bf16[48,768,256]{2,1,0:T(8,128)(2,1)S(1)} %get-tuple-element.5.m_ref, bf16[1,64,768]{2,1,0:T(8,128)(2,1)S(1)} %get-tuple-element.6.dx_ref), custom_call_target="tpu_custom_call" | custom-call | tf_op jit(solution)/shard_map/write_out/pallas_call | solution.py:618

commit v5 on v4

--- a/solution.py
+++ b/solution.py
@@ -13,7 +13,7 @@
 TILES = 3
 RING = 4
 RECV_RING = 8
-MOVED = (4, 1)
+MOVED = (4, 2, 1, 5)
 POS = 26
 HAND = 13
 EARLY = 10
@@ -171,7 +171,8 @@
             cot_arrival(t, n).wait_recv()
 
     def prepare(k, carry):
-        lt_s[k, 0] = jnp.concatenate([xs_s[t, k] for t in range(stages)], axis=0).T
+        kept = [xs_s[t, k] * (pp + t < stages).astype(BF16) for t in range(stages)]
+        lt_s[k, 0] = jnp.concatenate(kept, axis=0).T
         return carry
 
     def acts(part):
@@ -180,6 +181,7 @@
             q = i % nq
             hh = rm_s[k, COLS + q, 2 * part:2 * part + 2].reshape(2 * tok, cw).astype(F32)
             act, _ = gelu_and_slope(hh)
+            act = jnp.where(lax.broadcasted_iota(jnp.int32, act.shape, 0) < (stages - pp - 2 * part) * tok, act, 0.0)
             lt_s[k, 1 + q // COLS, pl.ds(pl.multiple_of((q % COLS) * cw, 128), cw), 2 * part * tok:2 * (part + 1) * tok] = act.astype(BF16).T
             return carry
         lax.fori_loop(0, 2 * nq, body, 0)
@@ -188,12 +190,24 @@
         zero = jnp.zeros((tok, cw), BF16)
 
         def one_layer(k, c2):
-            for j in range(COLS + nq):
+            for j in range(COLS):
                 rm_s[k, j, t] = zero
             return c2
         return lax.fori_loop(0, 2, one_layer, carry)
 
     last = stages - 1 - pp
+    uses_later = pp + 2 < stages
+
+    @pl.when(jnp.logical_not(uses_later))
+    def _():
+        def blank(i, carry):
+            k = i // nq
+            q = i % nq
+            rm_s[k, COLS + q, 2:] = jnp.zeros((stages - 2, tok, cw), BF16)
+            lt_s[k, 1 + q // COLS, pl.ds(pl.multiple_of((q % COLS) * cw, 128), cw), 2 * tok:] = jnp.zeros((cw, (stages - 2) * tok), BF16)
+            return carry
+        lax.fori_loop(0, 2 * nq, blank, 0)
+    lax.fori_loop(last + 1, stages, zero_inactive, 0)
     h_wait(0)
     w_out_copy(0).start()
     w_in_start(0)
@@ -208,39 +222,34 @@
     w_in_wait(0)
     layer(0, 0, True)
     acc_start(0, 0)
-    for part in range(1, stages // 2):
-        h_start(part)
+
+    @pl.when(uses_later)
+    def _():
+        h_start(1)
     x_copy.wait()
     lax.fori_loop(0, 2, prepare, 0)
-    for part in range(1, stages // 2):
-        h_wait(part)
+
+    @pl.when(uses_later)
+    def _():
+        h_wait(1)
 
     def middle(t, carry):
         cot_wait(t)
         layers(t)
-        for part in range(1, stages // 2):
-            @pl.when(t == 2 * part - 1)
-            def _():
-                acts(part)
+
+        @pl.when((t == 1) & uses_later)
+        def _():
+            acts(1)
         return carry
 
     lax.fori_loop(1, jnp.where(pp == 0, stages - 1, last + 1), middle, 0)
-
-    @pl.when(last == 0)
-    def _():
-        def blank(i, carry):
-            lt_s[1 - i // (1 + nb), i % (1 + nb), :, 2 * tok:] = jnp.zeros((hid, (stages - 2) * tok), BF16)
-            return carry
-        lax.fori_loop(0, 2 * (1 + nb), blank, 0)
-    lax.fori_loop(last + 1, stages, zero_inactive, 0)
 
     half = hid // 2
     hb = core * half
     xb = hb
     yb = hb + 4 * unit
-    zp = stages - 1 - pp
     helper = pp >= stages // 2
-    moved = jnp.where((pp == 0) | (pp == stages - 1), MOVED[0], MOVED[1])
+    moved = jnp.where(helper, jnp.where(pp == 2, MOVED[2], MOVED[3]), jnp.where(pp == 0, MOVED[0], MOVED[1]))
     steps = jnp.where(helper, total + moved, total - moved)
     own = jnp.where(helper, total, total - moved)
 
@@ -259,7 +268,8 @@
 
         def remote(src, dst, target):
             j = c if kind in (0, 9) else i
-            return pltpu.make_async_remote_copy(src_ref=src, dst_ref=dst, send_sem=send_sem.at[kind, j % RING], recv_sem=recv_sem.at[kind, j % RECV_RING], **dev(pp, target))
+            row = (kind + 1) // 2
+            return pltpu.make_async_remote_copy(src_ref=src, dst_ref=dst, send_sem=send_sem.at[row, j % RING], recv_sem=recv_sem.at[row, j % RECV_RING], **dev(pp, target))
 
         def place(start, n):
             return p_s.at[c, rows_of(start, n), :] if foreign else m_ref.at[c, rows_of(hb + start, n), :]
@@ -293,19 +303,49 @@
         r = m_ref.at[c, rows_of(half - hb if f else hb, half), :]
         return remote(r, r, pair)
 
+    def taker(f):
+        near = (pp == 1) & (f == 0)
+        return jnp.where(near, 2, 3), jnp.where(pp == 0, f, jnp.where(near, 0, MOVED[0]))
+
+    def giver(f):
+        far = (pp == 3) & (f < MOVED[0])
+        return jnp.where(far, 0, 1), jnp.where(far, f, jnp.where(pp == 3, 1, 0))
+
     def moved_msg(kind, f, arriving=False):
         c = total - moved + f
 
-        def remote(src, dst, pp_i, dp_i):
-            return pltpu.make_async_remote_copy(src_ref=src, dst_ref=dst, send_sem=mv_send.at[kind, f], recv_sem=mv_recv.at[kind, f], **dev(pp_i, dp_i))
+        def remote(src, dst, there, pp_i, dp_i):
+            return pltpu.make_async_remote_copy(src_ref=src, dst_ref=dst, send_sem=mv_send.at[int(kind % 3 > 0), f], recv_sem=mv_recv.at[int(kind % 3 > 0), there], **dev(pp_i, dp_i))
         if kind == 0:
-            return remote(m_ref.at[c, rows_of(half - hb, half), :], p_s.at[c], pp, pair)
+            return remote(m_ref.at[c, rows_of(half - hb, half), :], p_s.at[c], f, pp, pair)
         if kind == 1:
-            return remote(p_s.at[c], p_s.at[f], zp, dp)
+            if arriving:
+                return remote(p_s.at[f], p_s.at[f], f, giver(f)[0], dp)
+            stage, place = taker(f)
+            return remote(p_s.at[c], p_s.at[place], place, stage, dp)
         if kind == 2:
-            return remote(p_s.at[f], m_ref.at[c, rows_of(hb, half), :], zp, dp)
+            if arriving:
+                return remote(p_s.at[f], m_ref.at[c, rows_of(hb, half), :], f, taker(f)[0], dp)
+            stage, piece = giver(f)
+            there = total - jnp.where(stage == 0, MOVED[0], MOVED[1]) + piece
+            return remote(p_s.at[f], m_ref.at[there, rows_of(hb, half), :], piece, stage, dp)
         r = m_ref.at[c, rows_of(half - hb if arriving else hb, half), :]
-        return remote(r, r, pp, pair)
+        return remote(r, r, f, pp, pair)
+
+    def bytes_of(kind):
+        return {0: p_s, 1: h1_s, 3: h2_s, 5: h2_s, 7: h1_s, 9: p_s}[kind].at[0]
+
+    def wait_on(sem, kind):
+        place = bytes_of(kind)
+        pltpu.make_async_copy(place, place, sem).wait()
+
+    def wait_sent(kind, i):
+        j = own_of(i) if kind in (0, 9) else i
+        wait_on(send_sem.at[(kind + 1) // 2, j % RING], kind)
+
+    def arrive(kind, i):
+        j = own_of(i) if kind in (0, 9) else i
+        wait_on(recv_sem.at[(kind + 1) // 2, j % RECV_RING], kind)
 
     def send(kind, i, foreign):
         if kind >= 3:
@@ -315,12 +355,8 @@
             def _():
                 wait_sent(kind, i)
         msg(kind, i, foreign).start()
-
-    def wait_sent(kind, i):
-        msg(kind, i, False).wait_send()
-
-    def arrive(kind, i, foreign):
-        msg(kind, i, foreign, True).wait_recv()
+        if kind not in (0, 9):
+            msg(kind + 1, i, foreign).start()
 
     def plus(left, right):
         return (left.astype(F32) + right.astype(F32)).astype(BF16)
@@ -353,30 +389,26 @@
             f = i - POS
             moved_msg(1, f, True).wait_recv()
             send(1, i, True)
-            send(2, i, True)
             return
         c = own_of(i)
-        arrive(0, i, False)
+        arrive(0, i)
         p_s[c] = plus(p_s[c], m_ref[c, rows_of(hb, half), :])
         send(1, i, False)
-        send(2, i, False)
         wait_sent(0, i)
         pl.semaphore_signal(free_sem, inc=1, **dev(pp, pair))
 
     def stage2(i, foreign):
         c = i - POS if foreign else own_of(i)
-        arrive(1, i, foreign)
+        arrive(1, i)
         h1_s[c, 0] = plus(h1_s[c, 0], p_s[c, rows_of(xc * 2 * unit, 2 * unit), :])
-        wait_sent(2, i)
-        send(3, i, foreign)
-        arrive(2, i, foreign)
         h1_s[c, 1] = plus(h1_s[c, 1], p_s[c, rows_of(4 * unit + yc * 2 * unit, 2 * unit), :])
         wait_sent(1, i)
-        send(4, i, foreign)
+        send(3, i, foreign)
         if not foreign:
             @pl.when(helper & (i < moved))
             def _():
-                pl.semaphore_signal(z_free, inc=1, **dev(zp, dp))
+                stage, piece = giver(i)
+                pl.semaphore_signal(z_free.at[piece], inc=1, **dev(stage, dp))
 
     def stage3(i, foreign):
         c = i - POS if foreign else own_of(i)
@@ -386,22 +418,17 @@
                 p_s[c, rows_of(start, unit), :] = value
             else:
                 m_ref[c, rows_of(hb + start, unit), :] = value
-        arrive(3, i, foreign)
+        arrive(3, i)
         keep(xc * 2 * unit + yc * unit, plus(h1_s[c, 0, rows_of(yc * unit, unit), :], h2_s[c, 0]))
+        keep(4 * unit + yc * 2 * unit + xc * unit, plus(h1_s[c, 1, rows_of(xc * unit, unit), :], h2_s[c, 1]))
         send(5, i, foreign)
-        arrive(4, i, foreign)
-        keep(4 * unit + yc * 2 * unit + xc * unit, plus(h1_s[c, 1, rows_of(xc * unit, unit), :], h2_s[c, 1]))
-        send(6, i, foreign)
 
     def stage4(i, foreign):
-        arrive(5, i, foreign)
+        arrive(5, i)
         send(7, i, foreign)
-        arrive(6, i, foreign)
-        send(8, i, foreign)
 
     def stage5(i, foreign):
-        arrive(7, i, foreign)
-        arrive(8, i, foreign)
+        arrive(7, i)
         if foreign:
             moved_msg(2, i - POS).start()
             return
@@ -410,7 +437,7 @@
 
     def stage6(i, foreign):
         if not foreign:
-            arrive(9, i, False)
+            arrive(9, i)
 
     plan = ((stage6, 16), (stage5, 14), (stage4, 11), (stage3, 8), (stage2, 5), (stage1, 2), (produce, 0))
     depth = max(lag for _, lag in plan)
@@ -447,7 +474,7 @@
             p_s[c] = plus(p_s[c], m_ref[c, rows_of(hb, half), :])
             moved_msg(0, f).wait_send()
             pl.semaphore_signal(mv_free, inc=1, **dev(pp, pair))
-            pl.semaphore_wait(z_free, 1)
+            pl.semaphore_wait(z_free.at[f], 1)
             moved_msg(1, f).start()
 
     def give(i):
@@ -455,7 +482,7 @@
 
         @pl.when((f >= 0) & (f < moved))
         def _():
-            moved_msg(2, f).wait_recv()
+            moved_msg(2, f, True).wait_recv()
             pl.semaphore_wait(mv_free, 1)
             moved_msg(3, f).start()
 
@@ -496,8 +523,8 @@
         lax.fori_loop(0, moved, back, 0)
 
     def drain(i, carry):
-        for kind in range(3, 10):
-            msg(kind, steps - RING + i, False).wait_send()
+        for kind in (3, 5, 7, 9):
+            wait_sent(kind, steps - RING + i)
         return carry
 
     lax.fori_loop(0, RING, drain, 0)
@@ -604,12 +631,12 @@
                 pltpu.SemaphoreType.DMA((2,)),
                 pltpu.SemaphoreType.DMA((stages, TILES)),
                 pltpu.SemaphoreType.DMA((stages, TILES)),
-                pltpu.SemaphoreType.DMA((10, RING)),
-                pltpu.SemaphoreType.DMA((10, RECV_RING)),
+                pltpu.SemaphoreType.DMA((6, RING)),
+                pltpu.SemaphoreType.DMA((6, RECV_RING)),
                 pltpu.SemaphoreType.REGULAR,
-                pltpu.SemaphoreType.DMA((4, max(MOVED))),
-                pltpu.SemaphoreType.DMA((4, max(MOVED))),
-                pltpu.SemaphoreType.REGULAR,
+                pltpu.SemaphoreType.DMA((2, max(MOVED))),
+                pltpu.SemaphoreType.DMA((2, max(MOVED))),
+                pltpu.SemaphoreType.REGULAR((max(MOVED[:2]),)),
                 pltpu.SemaphoreType.REGULAR,
             ],
             compiler_params=pltpu.CompilerParams(collective_id=0, has_side_effects=True, vmem_limit_bytes=46900 * 1024),

time: 202 us -> 201 us (level)
  no operation moved by 1% of the time
where the time goes in v5:
time: 201 us; the launch traced here: 199 us
  Pallas kernels  198 us (99%)
    pallas_call x1, Pallas kernels, device_fn(): pl.pallas_call(functools.partial(main_kernel, sizes), out_shape=(pltpu.VM...  186 us
    pallas_call x1, Pallas kernels, device_fn(): pl.pallas_call(functools.partial(write_kernel, sizes), out_shape=(jax.Sha...  12.2 us

profile of v5, /device:TPU:0, one launch (start us, length us, event | category | flops | bytes accessed | tf_op | source)
XLA Modules:
  0.0 199.2 jit_solution(10076165358870862217)
XLA Ops:
  0.6 186.2 %chain_reduce.1 = (bf16[48,768,256]{2,1,0:T(8,128)(2,1)S(1)}, bf16[1,64,768]{2,1,0:T(8,128)(2,1)S(1)}) custom-call(bf16[1,2,768,3072]{3,2,1,0:T(8,128)(2,1)} %w_in.1, bf16[1,2,3072,768]{3,2,1,0:T(8,128)(2,1)} %w_out.1, bf16[1,4,2,64,768]{4,3,2,1,0:T(8,128)(2,1)} %x_saved.1, bf16[1,4,2,64,3072]{4,3,2,1,0:T(8,128)(2,1)} %h_saved.1, bf16[1,64,768]{2,1,0:T(8,128)(2,1)} %dy_in.1, ...), custom_call_target="tpu_custom_call" | custom-call | tf_op jit(solution)/shard_map/chain_reduce/pallas_call | solution.py:611
  186.8 12.2 %write_out.1 = (f32[1,2,768,3072]{3,2,1,0:T(8,128)}, f32[1,2,3072,768]{3,2,1,0:T(8,128)}, bf16[1,64,768]{2,1,0:T(8,128)(2,1)}) custom-call(bf16[48,768,256]{2,1,0:T(8,128)(2,1)S(1)} %get-tuple-element.5.m_ref, bf16[1,64,768]{2,1,0:T(8,128)(2,1)S(1)} %get-tuple-element.6.dx_ref), custom_call_target="tpu_custom_call" | custom-call | tf_op jit(solution)/shard_map/write_out/pallas_call | solution.py:645

commit v6 on v5

--- a/solution.py
+++ b/solution.py
@@ -13,10 +13,11 @@
 TILES = 3
 RING = 4
 RECV_RING = 8
-MOVED = (4, 2, 1, 5)
+MOVED = (3, 2, 1, 4)
 POS = 26
-HAND = 13
-EARLY = 10
+HAND = 16
+EARLY = (10, 15)
+AHEAD = 2
 
 
 def gelu_and_slope(h):
@@ -220,8 +221,9 @@
     x_copy.start()
     w_out_copy(0).wait()
     w_in_wait(0)
+    for c in range(AHEAD):
+        acc_start(c, c)
     layer(0, 0, True)
-    acc_start(0, 0)
 
     @pl.when(uses_later)
     def _():
@@ -377,11 +379,11 @@
             return
         c = own_of(i)
 
-        @pl.when(c + 1 < own)
-        def _():
-            acc_start(c + 1, (c + 1) % 2)
-        acc_wait(c % 2)
-        product(c, c % 2)
+        @pl.when(c + AHEAD < own)
+        def _():
+            acc_start(c + AHEAD, (c + AHEAD) % (AHEAD + 1))
+        acc_wait(c % (AHEAD + 1))
+        product(c, c % (AHEAD + 1))
         send(0, i, False)
 
     def stage1(i, foreign):
@@ -461,9 +463,9 @@
         def _():
             f = i - HAND
             c = total - moved + f
-            acc_start(c, i % 2)
-            acc_wait(i % 2)
-            product(c, i % 2)
+            acc_start(c, i % (AHEAD + 1))
+            acc_wait(i % (AHEAD + 1))
+            product(c, i % (AHEAD + 1))
             moved_msg(0, f).start()
 
         @pl.when((i >= HAND + 2) & (i < HAND + 2 + moved))
@@ -489,9 +491,13 @@
     def step(i, carry):
         @pl.when(pp == 0)
         def _():
-            @pl.when(i == EARLY)
+            @pl.when(i == EARLY[0])
             def _():
-                layers(jnp.int32(stages - 1))
+                layer(jnp.int32(stages - 1), 1, False)
+
+            @pl.when(i == EARLY[1])
+            def _():
+                layer(jnp.int32(stages - 1), 0, True)
         run(i)
 
         @pl.when(jnp.logical_not(helper))
@@ -620,7 +626,7 @@
                 pltpu.VMEM((2, COLS + nq, stages, tok, cw), BF16),
                 pltpu.VMEM((stages, 2, tok, hid), BF16),
                 pltpu.VMEM((stages, TILES, tok, hid // TILES), BF16),
-                pltpu.VMEM((2, hid, cw), F32),
+                pltpu.VMEM((AHEAD + 1, hid, cw), F32),
                 pltpu.VMEM((total, hid // 2, cw), BF16),
                 pltpu.VMEM((total, 2, 2 * unit, cw), BF16),
                 pltpu.VMEM((total, 2, unit, cw), BF16),
@@ -628,7 +634,7 @@
                 pltpu.SemaphoreType.DMA((stages // 2,)),
                 pltpu.SemaphoreType.DMA,
                 pltpu.SemaphoreType.DMA,
-                pltpu.SemaphoreType.DMA((2,)),
+                pltpu.SemaphoreType.DMA((AHEAD + 1,)),
                 pltpu.SemaphoreType.DMA((stages, TILES)),
                 pltpu.SemaphoreType.DMA((stages, TILES)),
                 pltpu.SemaphoreType.DMA((6, RING)),

time: 201 us -> 200 us (level)
  no operation moved by 1% of the time
where the time goes in v6:
time: 200 us
  Pallas kernels  199 us (100%)
    pallas_call x1, Pallas kernels, device_fn(): pl.pallas_call(functools.partial(main_kernel, sizes), out_shape=(pltpu.VM...  186 us
    pallas_call x1, Pallas kernels, device_fn(): pl.pallas_call(functools.partial(write_kernel, sizes), out_shape=(jax.Sha...  12.2 us

profile of v6, /device:TPU:0, one launch (start us, length us, event | category | flops | bytes accessed | tf_op | source)
XLA Modules:
  0.0 199.5 jit_solution(6331398160082397557)
XLA Ops:
  0.6 186.5 %chain_reduce.1 = (bf16[48,768,256]{2,1,0:T(8,128)(2,1)S(1)}, bf16[1,64,768]{2,1,0:T(8,128)(2,1)S(1)}) custom-call(bf16[1,2,768,3072]{3,2,1,0:T(8,128)(2,1)} %w_in.1, bf16[1,2,3072,768]{3,2,1,0:T(8,128)(2,1)} %w_out.1, bf16[1,4,2,64,768]{4,3,2,1,0:T(8,128)(2,1)} %x_saved.1, bf16[1,4,2,64,3072]{4,3,2,1,0:T(8,128)(2,1)} %h_saved.1, bf16[1,64,768]{2,1,0:T(8,128)(2,1)} %dy_in.1, ...), custom_call_target="tpu_custom_call" | custom-call | tf_op jit(solution)/shard_map/chain_reduce/pallas_call | solution.py:617
  187.1 12.2 %write_out.1 = (f32[1,2,768,3072]{3,2,1,0:T(8,128)}, f32[1,2,3072,768]{3,2,1,0:T(8,128)}, bf16[1,64,768]{2,1,0:T(8,128)(2,1)}) custom-call(bf16[48,768,256]{2,1,0:T(8,128)(2,1)S(1)} %get-tuple-element.5.m_ref, bf16[1,64,768]{2,1,0:T(8,128)(2,1)S(1)} %get-tuple-element.6.dx_ref), custom_call_target="tpu_custom_call" | custom-call | tf_op jit(solution)/shard_map/write_out/pallas_call | solution.py:651

commit v7 on v6

--- a/solution.py
+++ b/solution.py
@@ -14,8 +14,8 @@
 RING = 4
 RECV_RING = 8
 MOVED = (3, 2, 1, 4)
-POS = 26
-HAND = 16
+POS = 34
+HAND = 20
 EARLY = (10, 15)
 AHEAD = 2
 

time: 200 us -> 200 us (level)
  no operation moved by 1% of the time
where the time goes in v7:
time: 200 us
  Pallas kernels  199 us (100%)
    pallas_call x1, Pallas kernels, device_fn(): pl.pallas_call(functools.partial(main_kernel, sizes), out_shape=(pltpu.VM...  186 us
    pallas_call x1, Pallas kernels, device_fn(): pl.pallas_call(functools.partial(write_kernel, sizes), out_shape=(jax.Sha...  12.2 us

profile of v7, /device:TPU:0, one launch (start us, length us, event | category | flops | bytes accessed | tf_op | source)
XLA Modules:
  0.0 199.5 jit_solution(694793087314859106)
XLA Ops:
  0.6 186.5 %chain_reduce.1 = (bf16[48,768,256]{2,1,0:T(8,128)(2,1)S(1)}, bf16[1,64,768]{2,1,0:T(8,128)(2,1)S(1)}) custom-call(bf16[1,2,768,3072]{3,2,1,0:T(8,128)(2,1)} %w_in.1, bf16[1,2,3072,768]{3,2,1,0:T(8,128)(2,1)} %w_out.1, bf16[1,4,2,64,768]{4,3,2,1,0:T(8,128)(2,1)} %x_saved.1, bf16[1,4,2,64,3072]{4,3,2,1,0:T(8,128)(2,1)} %h_saved.1, bf16[1,64,768]{2,1,0:T(8,128)(2,1)} %dy_in.1, ...), custom_call_target="tpu_custom_call" | custom-call | tf_op jit(solution)/shard_map/chain_reduce/pallas_call | solution.py:617
  187.1 12.2 %write_out.1 = (f32[1,2,768,3072]{3,2,1,0:T(8,128)}, f32[1,2,3072,768]{3,2,1,0:T(8,128)}, bf16[1,64,768]{2,1,0:T(8,128)(2,1)}) custom-call(bf16[48,768,256]{2,1,0:T(8,128)(2,1)S(1)} %get-tuple-element.5.m_ref, bf16[1,64,768]{2,1,0:T(8,128)(2,1)S(1)} %get-tuple-element.6.dx_ref), custom_call_target="tpu_custom_call" | custom-call | tf_op jit(solution)/shard_map/write_out/pallas_call | solution.py:651
